TPU v7x, 128 devices: a whole 4x4x4 slice. The times are simulated.
128 devices in a mesh: dp: 8 (over y, x_hi), expert: 16 (over z, x_lo, core).
Axes of the slice: x: 4 (x_hi: 2, x_lo: 2; x = x_hi * 2 + x_lo), y: 4, z: 4, core: 2. Of those that a mesh axis runs over, the one named last changes fastest.
Arguments:
- expert_ids: int32 [4096, 8], P(('dp', 'expert')), may hold values from 0 to 15, all different within a row; in each aligned block of 32 rows (0 to 31, 32 to 63, ...) at most 20 rows name the same one
- expert_home: int32 [16], replicated, may hold values from 0 to 15, each once
- live_tokens: int32 [128], P(('dp', 'expert')), may hold values from 1 to 32, 3072 in all
- gate_weights: float32 [4096, 8], P(('dp', 'expert')), may hold values from 0.1 to 1
- output_grad: bfloat16 [4096, 7168], P(('dp', 'expert')), may hold values from -6 to 6
- saved_hidden: bfloat16 [4096, 8, 1024], P(('dp', 'expert')), may hold values from -2.5 to 2.5
- down_weight: bfloat16 [16, 1024, 7168], P('expert'), may hold values from -0.1875 to 0.1875
- dense_input: bfloat16 [4096, 7168], P(('dp', 'expert')), may hold values from -24 to 24
- latent_grad: bfloat16 [4096, 256], P(('dp', 'expert')), may hold values from -0.09375 to 0.09375
Outputs:
- hidden_grad: bfloat16 [4096, 8, 1024], P(('dp', 'expert'))
- expert_grad: float32 [16, 1024, 7168], P('expert', 'dp')
- dense_grad: float32 [7168, 256], P(('dp', 'expert'))
Inputs may be any that keep to these rules, and one draw needn't show every extreme that they name: `expert_ids`: each row names 8 different experts. Among the rows of one device no expert is named more than 20 times, and on some devices one expert is named exactly 20 times. A permutation: expert e is held at index expert_home[e] of the expert axis, in every dp replica. `live_tokens`: entry i is the number of real tokens at the start of device i, in the order of the joined dp and expert axes; the rest are padding. Some device has all 32 real.
All inputs are finite; a program needn't handle non-finite values.
Results may differ from a plain program's by a relative error of at most 0.008.
Values may be sent and summed in bfloat16 or wider, within the bound.
A program may use at most 192 MiB of HBM per device.

v0:
```python
import jax
import jax.numpy as jnp
from jax import lax
from jax.sharding import Mesh
from jax.sharding import PartitionSpec as P

DP = ("dp_0", "dp_1")
EXPERT = ("expert_0", "expert_1", "expert_2")
DP_EXPERT = ("dp_0", "dp_1", "expert_0", "expert_1", "expert_2")


def split_up(shard, dim, size):
    dims = shard.shape
    blocks = shard.reshape(*dims[:dim], size, dims[dim] // size, *dims[dim + 1 :])
    return jnp.moveaxis(blocks, dim, 0)


def in_order(blocks, dim):
    blocks = jnp.moveaxis(blocks, 0, dim)
    dims = blocks.shape
    return blocks.reshape(*dims[:dim], dims[dim] * dims[dim + 1], *dims[dim + 2 :])


def moved_by_axis(blocks, axes, sequence):
    inside = blocks.shape[1:]
    result = blocks.reshape(*(lax.axis_size(a) for a in axes), *inside)
    for k in sequence:
        result = lax.all_to_all(result, axes[k], k, k, tiled=True)
    return result.reshape(-1, *inside)


def two_step_exchange(shard, groups, sequence, split_dim, concat_dim):
    size = lax.axis_size(groups[0]) * lax.axis_size(groups[1])
    blocks = split_up(shard, split_dim, size)
    return in_order(moved_by_axis(blocks, groups, sequence), concat_dim)


def side_by_side(arrays, axis, split_dim, concat_dim, along):
    both = jnp.concatenate(arrays, axis=along)
    result, at, gathered = (
        lax.all_to_all(both, axis, split_axis=split_dim, concat_axis=concat_dim, tiled=True),
        0,
        [],
    )
    for a in arrays:
        gathered.append(lax.slice_in_dim(result, at, at + a.shape[along], axis=along))
        at += a.shape[along]
    return tuple(gathered)


def on_device(
    expert_ids,
    expert_home,
    live_tokens,
    gate_weights,
    output_grad,
    saved_hidden,
    down_weight,
    dense_input,
    latent_grad,
):
    n_group = lax.axis_size(EXPERT)
    tok_rows, top_count = expert_ids.shape
    model_width = output_grad.shape[1]
    hidden_units = saved_hidden.shape[2]
    capacity = tok_rows * top_count * 5 // (4 * n_group)
    is_live = jnp.arange(tok_rows, dtype=jnp.int32) < live_tokens[0]
    masked_grad = jnp.where(is_live[:, None], latent_grad, jnp.zeros_like(latent_grad))
    owned_columns = two_step_exchange(
        dense_input, (("dp_0", "dp_1", "expert_0", "expert_1"), "expert_2"), (1, 0), 1, 0
    )
    dense_grad = lax.dot_general(
        owned_columns,
        lax.all_gather(masked_grad, DP_EXPERT, axis=0, tiled=True),
        (((0,), (0,)), ((), ())),
        preferred_element_type=jnp.float32,
    )
    pair_count = tok_rows * top_count
    flat_ids = expert_ids.reshape(pair_count)
    expert_count = expert_home.shape[0]
    id_table = (flat_ids[:, None] == jnp.arange(expert_count, dtype=jnp.int32)[None, :]).astype(
        jnp.int32
    )
    home_slot = jnp.sum(id_table * expert_home[None, :], axis=1)
    slot_table = (home_slot[:, None] == jnp.arange(n_group, dtype=jnp.int32)[None, :]).astype(
        jnp.int32
    )
    earlier = jnp.cumsum(slot_table, axis=0) - slot_table
    position = jnp.sum(earlier * slot_table, axis=1)
    slot_index = home_slot * capacity + position
    pair_ids = jnp.arange(pair_count, dtype=jnp.int32)
    source_pair = jnp.zeros((n_group * capacity,), jnp.int32).at[slot_index].set(pair_ids)
    filled = jnp.zeros((n_group * capacity,), jnp.bool_).at[slot_index].set(True)
    source_token = source_pair // top_count
    pair_scale = (gate_weights * is_live[:, None].astype(jnp.float32)).reshape(pair_count)
    slot_scale = jnp.where(filled, pair_scale[source_pair], jnp.float32(0.0))
    grad_rows = (output_grad[source_token].astype(jnp.float32) * slot_scale[:, None]).astype(
        jnp.bfloat16
    )
    flat_hidden = saved_hidden.reshape(pair_count, hidden_units)
    hidden_rows = jnp.where(filled[:, None], flat_hidden[source_pair], jnp.zeros((), jnp.bfloat16))
    arrived_grad, arrived_hidden = side_by_side(
        (
            grad_rows.reshape(n_group, capacity, model_width),
            hidden_rows.reshape(n_group, capacity, hidden_units),
        ),
        EXPERT,
        0,
        0,
        2,
    )
    arrived_grad = arrived_grad.reshape(n_group * capacity, model_width)
    arrived_hidden = arrived_hidden.reshape(n_group * capacity, hidden_units)
    expert_weight = down_weight[0]
    input_grad = lax.dot_general(
        arrived_grad, expert_weight, (((1,), (1,)), ((), ())), preferred_element_type=jnp.float32
    ).astype(jnp.bfloat16)
    returned = two_step_exchange(
        input_grad.reshape(n_group, capacity, hidden_units),
        (("expert_0", "expert_1"), "expert_2"),
        (1, 0),
        0,
        0,
    )
    expert_grad = lax.psum_scatter(
        lax.dot_general(
            arrived_hidden,
            arrived_grad,
            (((0,), (0,)), ((), ())),
            preferred_element_type=jnp.float32,
        ),
        DP,
        scatter_dimension=0,
        tiled=True,
    )
    hidden_grad = returned.reshape(n_group * capacity, hidden_units)[slot_index].reshape(
        tok_rows, top_count, hidden_units
    )
    return (hidden_grad, expert_grad[None], dense_grad)


def solution(mesh):
    torus = Mesh(
        mesh.devices.reshape(4, 2, 4, 2, 2), ("dp_0", "dp_1", "expert_0", "expert_1", "expert_2")
    )
    in_specs = (
        P(DP_EXPERT, None),
        P(),
        P(DP_EXPERT),
        P(DP_EXPERT, None),
        P(DP_EXPERT, None),
        P(DP_EXPERT, None, None),
        P(EXPERT, None, None),
        P(DP_EXPERT, None),
        P(DP_EXPERT, None),
    )
    out_specs = (P(DP_EXPERT, None, None), P(EXPERT, DP, None), P(DP_EXPERT, None))
    return jax.shard_map(
        on_device, mesh=torus, in_specs=in_specs, out_specs=out_specs, check_vma=False
    )
```

profile of v0, /device:TPU:0, one launch (start us, length us, event | category | flops | bytes accessed | tf_op | source)
XLA Modules:
  0.0 501.9 jit_solution(9455983698504204111)
XLA Ops:
  8.0 0.0 copy-start
  8.0 0.0 copy-start.2
  8.0 0.8 copy.24
  8.9 0.1 eq.38
  9.0 0.7 select_reduce_fusion
  9.7 0.6 reduce-window.6
  10.3 0.2 slice_reduce_fusion
  10.5 0.1 fusion.8
  10.6 1.4 scatter_custom_fusion
  12.1 0.0 copy-done
  12.1 2.1 gather_fusion.2
  14.2 0.1 gather.17
  14.3 1.5 scatter_custom_fusion.1
  15.8 0.1 broadcast_in_dim.61
  15.9 0.0 copy-done.2
  15.9 6.1 %gather_fusion = bf16[320,7168]{1,0:T(8,128)(2,1)} fusion(bf16[32,7168]{1,0:T(8,128)(2,1)S(1)} %copy-done.2, s32[1024]{0:T(1024)S(1)} %get-tuple-element.6), kind=kCustom, calls=%fused_computation | custom fusion | bytes 9176320 | tf_op jit(solution)/shard_map/gather | solution.py:97
  22.1 0.0 copy-start.5
  22.1 8.1 %reshape.102 = f32[16,20,7168]{2,1,0:T(8,128)} reshape(bf16[320,7168]{1,0:T(8,128)(2,1)} %gather_fusion) | data formatting | bytes 13762560 | tf_op jit(solution)/shard_map/convert_element_type | solution.py:97
  30.8 0.0 copy-done.5
  30.8 0.1 copy.26
  30.9 0.1 reshape.96
  31.0 2.5 gather_fusion.1
  33.5 0.1 mul.51
  33.6 0.1 broadcast_select_fusion
  33.7 5.6 %multiply_convert_fusion = bf16[16,20,7168]{2,1,0:T(8,128)(2,1)S(1)} fusion(f32[16,20,7168]{2,1,0:T(8,128)} %reshape.102, f32[16,20]{1,0:T(8,128)S(1)} %mul.51), kind=kLoop, calls=%fused_computation.9 | loop fusion | flops 4587520 | bytes 13763840 | tf_op jit(solution)/shard_map/convert_element_type | solution.py:97
  39.3 3.3 pad_maximum_fusion
  42.7 0.0 copy-start.4
  42.7 6.6 %all-to-all-start = ((bf16[16,20,8192]{2,1,0:T(8,128)(2,1)}), bf16[16,20,8192]{2,1,0:T(8,128)(2,1)}, u32[]{:S(2)}, u32[]{:S(2)}) async-start(bf16[16,20,8192]{2,1,0:T(8,128)(2,1)} %pad_maximum_fusion), calls=%async_computation | async-start | bytes 12582912 | tf_op jit(solution)/shard_map/all_to_all | solution.py:41
  49.3 0.0 all-gather.2.cloned.1.call-start
  49.4 0.0 copy-done.4
  49.4 0.7 broadcast_select_fusion.1
  50.1 0.0 all-gather.2.cloned.1.call-update
  50.1 0.2 reduce-scatter.2.cloned.1.call-start
  50.3 73.3 %all-to-all-done = bf16[16,20,8192]{2,1,0:T(8,128)(2,1)} async-done(((bf16[16,20,8192]{2,1,0:T(8,128)(2,1)}), bf16[16,20,8192]{2,1,0:T(8,128)(2,1)}, u32[]{:S(2)}, u32[]{:S(2)}) %all-to-all-start) | async-done | bytes 5242912 | tf_op jit(solution)/shard_map/all_to_all | solution.py:41
  123.6 15.7 %convolution_bitcast_fusion = f32[1024,7168]{1,0:T(8,128)} fusion(bf16[16,20,8192]{2,1,0:T(8,128)(2,1)} %all-to-all-done), kind=kOutput, calls=%fused_computation.6 | convolution fusion | flops 4697620480 | bytes 34603008 | tf_op jit(solution)/shard_map/dot_general | solution.py:126
  139.3 0.0 copy-start.3
  139.3 0.0 reduce-scatter.2.cloned.1.call-update
  139.3 1.0 copy-done.3
  140.3 2.1 reshape.100
  142.4 0.9 copy.30
  143.3 0.8 reshape.160
  144.1 4.1 all_to_all.25
  148.2 0.7 reshape.161
  148.9 1.7 copy.31
  150.5 2.6 reshape.162
  153.2 5.3 %slice.25 = bf16[16,20,7168]{2,1,0:T(8,128)(2,1)} slice(bf16[16,20,8192]{2,1,0:T(8,128)(2,1)} %all-to-all-done), slice={[0:16], [0:20], [0:7168]} | slice | bytes 9175040 | tf_op jit(solution)/shard_map/slice | solution.py:46
  158.5 7.3 %reshape.98 = bf16[320,7168]{1,0:T(8,128)(2,1)} reshape(bf16[16,20,7168]{2,1,0:T(8,128)(2,1)} %slice.25) | data formatting | bytes 9175040 | tf_op jit(solution)/shard_map/reshape | solution.py:112
  165.8 11.6 %fusion.2 = bf16[320,1024]{1,0:T(8,128)(2,1)S(1)} fusion(bf16[320,7168]{1,0:T(8,128)(2,1)} %reshape.98, bf16[1,1024,7168]{2,1,0:T(8,128)(2,1)} %param.15), kind=kOutput, calls=%fused_computation.11 | convolution fusion | flops 4697948160 | bytes 19922944 | tf_op jit(solution)/shard_map/dot_general | solution.py:115
  177.4 0.1 reshape_reshape_reshape.6
  177.5 0.4 copy.27
  177.9 4.3 all_to_all.26
  182.2 9.6 %all-to-all-start.4 = ((bf16[64,2,1792]{2,1,0:T(2,128)(2,1)}), bf16[64,2,1792]{2,1,0:T(2,128)(2,1)S(1)}, u32[]{:S(2)}, u32[]{:S(2)}) async-start(bf16[64,2,1792]{2,1,0:T(2,128)(2,1)} %reshape.162), calls=%async_computation.5 | async-start | bytes 917504 | tf_op jit(solution)/shard_map/all_to_all | solution.py:28
  191.7 1.5 copy.28
  193.3 15.7 %all-to-all-done.4 = bf16[64,2,1792]{2,1,0:T(2,128)(2,1)S(1)} async-done(((bf16[64,2,1792]{2,1,0:T(2,128)(2,1)}), bf16[64,2,1792]{2,1,0:T(2,128)(2,1)S(1)}, u32[]{:S(2)}, u32[]{:S(2)}) %all-to-all-start.4) | async-done | bytes 458784 | tf_op jit(solution)/shard_map/all_to_all | solution.py:28
  209.0 3.8 all-to-all-start.2
  212.8 0.0 copy-start.1
  212.8 1.9 reshape.163
  214.7 274.7 %all-gather.2.cloned.1.call-done = bf16[4096,256]{1,0:T(8,128)(2,1)} async-done(((bf16[32,256]{1,0:T(8,128)(2,1)}), bf16[4096,256]{1,0:T(8,128)(2,1)}) %all-gather.2.cloned.1.call-update) | async-done | bytes 2097168 | tf_op jit(solution)/shard_map/all_gather | solution.py:74
  489.4 2.7 convolution_bitcast_fusion.1
  492.1 0.0 all-to-all-done.2
  492.1 0.2 copy.29
  492.3 0.1 reshape_reshape_reshape.7
  492.5 2.0 gather_fusion.3
  494.4 0.0 copy-done.1
  (15 shorter events, 0.1 us)
Async XLA Ops:
  8.0 4.1 copy-start
  8.0 7.9 %copy-start.2 = (bf16[32,7168]{1,0:T(8,128)(2,1)S(1)}, bf16[32,7168]{1,0:T(8,128)(2,1)}, u32[]{:S(2)}) copy-start(bf16[32,7168]{1,0:T(8,128)(2,1)} %param.13) | copy-start | bytes 1376260
  22.1 8.7 %copy-start.5 = (f32[32,8]{0,1:T(8,128)S(1)}, f32[32,8]{0,1:T(8,128)}, u32[]{:S(2)}) copy-start(f32[32,8]{0,1:T(8,128)} %param.12) | copy-start | bytes 3076
  42.7 6.7 %copy-start.4 = (bf16[32,256]{1,0:T(8,128)(2,1)S(1)}, bf16[32,256]{1,0:T(8,128)(2,1)}, u32[]{:S(2)}) copy-start(bf16[32,256]{1,0:T(8,128)(2,1)} %param.17) | copy-start | bytes 49156
  42.7 81.0 %all-to-all-start = ((bf16[16,20,8192]{2,1,0:T(8,128)(2,1)}), bf16[16,20,8192]{2,1,0:T(8,128)(2,1)}, u32[]{:S(2)}, u32[]{:S(2)}) async-start(bf16[16,20,8192]{2,1,0:T(8,128)(2,1)} %pad_maximum_fusion), calls=%async_computation | async-start | bytes 12582912 | tf_op jit(solution)/shard_map/all_to_all | solution.py:41
  49.3 440.1 %all-gather.2.cloned.1.call-start = ((), (), s32[]{:S(2)}) async-start(), calls=%async_computation.7 | async-start | bytes 2113536 | tf_op jit(solution)/shard_map/all_gather | solution.py:74
  50.1 444.3 %reduce-scatter.2.cloned.1.call-start = ((), (), s32[]{:S(2)}) async-start(), calls=%async_computation.6 | async-start | bytes 33030144 | tf_op jit(solution)/shard_map/reduce_scatter | solution.py:125
  139.3 1.0 copy-start.3
  182.2 26.9 %all-to-all-start.4 = ((bf16[64,2,1792]{2,1,0:T(2,128)(2,1)}), bf16[64,2,1792]{2,1,0:T(2,128)(2,1)S(1)}, u32[]{:S(2)}, u32[]{:S(2)}) async-start(bf16[64,2,1792]{2,1,0:T(2,128)(2,1)} %reshape.162), calls=%async_computation.5 | async-start | bytes 917504 | tf_op jit(solution)/shard_map/all_to_all | solution.py:28
  209.0 283.1 %all-to-all-start.2 = ((bf16[8,2,1,20,1024]{4,1,3,2,0:T(2,128)(2,1)}), bf16[8,2,1,20,1024]{4,1,3,2,0:T(2,128)(2,1)S(1)}, u32[]{:S(2)}, u32[]{:S(2)}) async-start(bf16[8,2,1,20,1024]{4,1,3,2,0:T(2,128)(2,1)} %copy.28), calls=%async_computation.2 | async-start | bytes 1310720 | tf_op jit(solution)/shard_map/all_to_all | solution.py:28
  212.8 281.6 %copy-start.1 = (bf16[32,8,1024]{2,1,0:T(8,128)(2,1)S(1)}, bf16[32,8,1024]{2,1,0:T(8,128)(2,1)}, u32[]{:S(2)}) copy-start(bf16[32,8,1024]{2,1,0:T(8,128)(2,1)} %param.14) | copy-start | bytes 1572868
Sparse Core Ops, SparseCore 0:
  52.4 436.9 all-gather.1
Sparse Core Ops, SparseCore 1:
  139.4 311.1 reduce-scatter.1
where the time goes:
time: 504 us; the launch traced here: 502 us
  waiting for transfers between devices  364 us (72%)
  local copies, waits for them, and re-layouts  51.8 us (10%)
  matrix products  30 us (6%)
  starting transfers between devices  20.3 us (4%)
  between operations  16.4 us (3%)
  other arithmetic  11.3 us (2%)
  blocking collectives  8.37 us (2%)
    all_gather x1, waiting for transfers between devices, on_device(): lax.all_gather(masked_grad, DP_EXPERT, axis=0, tiled=True)  275 us
    all_to_all x1, waiting for transfers between devices, side_by_side(): lax.all_to_all(both, axis, split_axis=split_dim, concat_axis=concat_dim,...  73.3 us
    all_to_all x2, waiting for transfers between devices, moved_by_axis(): result = lax.all_to_all(result, axes[k], k, k, tiled=True)  15.7 us
    dot_general x1, matrix products, on_device(): lax.dot_general(arrived_hidden, arrived_grad, (((0,), (0,)), ((), ())), p...  15.7 us
    all_to_all x2, starting transfers between devices, moved_by_axis(): result = lax.all_to_all(result, axes[k], k, k, tiled=True)  13.4 us
    dot_general x1, matrix products, on_device(): lax.dot_general(arrived_grad, expert_weight, (((1,), (1,)), ((), ())), pr...  11.6 us
  transfers between devices with their start and end apart: 5, of which 3 were waited for; matrix products, arithmetic and copies ran while one was open for 12% of the time, Pallas kernels for 0%

commit v1 on v0

v1 whole, which is shorter than its diff:
```python
import functools

import jax
import jax.numpy as jnp
from jax import lax
from jax.experimental import pallas as pl
from jax.experimental.pallas import tpu as pltpu
from jax.sharding import Mesh
from jax.sharding import PartitionSpec as P

DP = ("y", "xh")
EXPERT = ("z", "xl", "c")
ALL = ("y", "xh", "z", "xl", "c")
MESH = pl.DeviceIdType.MESH
NY, NX, NZ, NCORE, NXH, NXL = 4, 4, 4, 2, 2, 2
BF = jnp.bfloat16
F32 = jnp.float32
N_CHUNK = 4


def kernel(
    g_hbm,
    hs_hbm,
    w_hbm,
    x_hbm,
    lat_hbm,
    r_out,
    eg_out,
    dg_out,
    gbuf,
    hbuf,
    ht,
    wbuf,
    acch,
    hret,
    rbuf,
    part,
    own,
    relay,
    recv_p,
    recv_m,
    xbuf,
    lbuf,
    dpart,
    drecv,
    a1_s,
    a1_r,
    a2_s,
    a2_r,
    b1_s,
    b1_r,
    b2_s,
    b2_r,
    dd_s,
    dd_r,
    h_s,
    h_r,
    rs_s,
    rs_r,
    hr_s,
    hr_r,
    dx_s,
    dx_r,
    dl_s,
    dl_r,
    ds_s,
    ds_r,
    loc,
    w_sem,
    o_sem,
):
    y = lax.axis_index("y")
    xh = lax.axis_index("xh")
    z = lax.axis_index("z")
    xl = lax.axis_index("xl")
    c = lax.axis_index("c")
    x = xh * NXL + xl
    slot = z * 4 + xl * 2 + c
    dp = y * 2 + xh
    tok = g_hbm.shape[0]
    half_tok = tok // 2
    chunk = gbuf.shape[-1]
    half = chunk // 2
    frows = ht.shape[0] // NY
    hrow = frows // 2
    hid = w_hbm.shape[0]
    dcols = xbuf.shape[-1]
    drows = drecv.shape[1]

    def up(v, k, n):
        return lax.rem(v + k, n)

    def at_x(v):
        return {"xh": v // NXL, "xl": lax.rem(v, NXL)}

    xp, xm, x2 = up(x, 1, NX), up(x, NX - 1, NX), up(x, 2, NX)
    zp, zm, z2 = up(z, 1, NZ), up(z, NZ - 1, NZ), up(z, 2, NZ)
    yp, ym = up(y, 1, NY), up(y, NY - 1, NY)
    dev_x = (at_x(xp), at_x(xm))
    dev_z = ({"z": zp}, {"z": zm})
    dev_y = ({"y": yp}, {"y": ym})
    sibling = {"c": 1 - c}
    sent = []

    def remote(src, dst, ss, rs, dev):
        return pltpu.make_async_remote_copy(
            src_ref=src, dst_ref=dst, send_sem=ss, recv_sem=rs, device_id=dev, device_id_type=MESH
        )

    def send(src, dst, ss, rs, dev):
        d = remote(src, dst, ss, rs, dev)
        d.start()
        sent.append(d)

    def arrived(ref, ss, rs, dev):
        remote(ref, ref, ss, rs, dev).wait_recv()

    def lanes(h):
        return pl.ds(h * half, half)

    def own_copy(ch):
        return pltpu.make_async_copy(
            g_hbm.at[:, pl.ds(ch * chunk, chunk)], gbuf.at[ch, x, c, z], loc.at[ch]
        )

    def s0(ch):
        own_copy(ch).start()
        for h in range(2):
            src = g_hbm.at[:, pl.ds(ch * chunk + h * half, half)]
            dst = gbuf.at[ch, x, c, z, :, lanes(h)]
            for s in range(2):
                i = h * 2 + s
                send(src, dst, a1_s.at[ch, i], a1_r.at[ch, i], (dev_x, dev_z)[h][s])

    rows_of = (pl.ds(0, half_tok), pl.ds(half_tok, half_tok))

    def s1(ch):
        for h in range(2):
            for s in range(2):
                i = h * 2 + s
                if h == 0:
                    blk = gbuf.at[ch, (xm, xp)[s], c, z]
                else:
                    blk = gbuf.at[ch, x, c, (zm, zp)[s]]
                dev = (dev_x, dev_z)[h][s]
                arrived(blk.at[:, lanes(h)], a1_s.at[ch, i], a1_r.at[ch, i], dev)
                ref = blk.at[rows_of[s], lanes(h)]
                send(ref, ref, a2_s.at[ch, i], a2_r.at[ch, i], dev)

    def line(ch, h, other):
        if h == 0:
            return gbuf.at[ch, :, c, other, :, lanes(0)]
        return gbuf.at[ch, other, c, :, :, lanes(1)]

    def line_half(ch, h, other, s):
        if h == 0:
            return gbuf.at[ch, :, c, other, rows_of[s], lanes(0)]
        return gbuf.at[ch, other, c, :, rows_of[s], lanes(1)]

    def s2(ch):
        own_copy(ch).wait()
        for h in range(2):
            for s in range(2):
                i = h * 2 + s
                blk = gbuf.at[ch, x2, c, z] if h == 0 else gbuf.at[ch, x, c, z2]
                arrived(
                    blk.at[rows_of[s], lanes(h)],
                    a2_s.at[ch, i],
                    a2_r.at[ch, i],
                    (dev_x, dev_z)[h][s],
                )
            ref = line(ch, h, (z, x)[h])
            for s in range(2):
                i = h * 2 + s
                send(ref, ref, b1_s.at[ch, i], b1_r.at[ch, i], (dev_z, dev_x)[h][s])
            send(ref, ref, dd_s.at[ch, h], dd_r.at[ch, h], sibling)

    def s3(ch):
        for h in range(2):
            for s in range(2):
                i = h * 2 + s
                other = ((zm, zp), (xm, xp))[h][s]
                dev = (dev_z, dev_x)[h][s]
                ref = line(ch, h, other)
                arrived(ref, b1_s.at[ch, i], b1_r.at[ch, i], dev)
                fwd = line_half(ch, h, other, s)
                send(fwd, fwd, b2_s.at[ch, i], b2_r.at[ch, i], dev)
                send(ref, ref, dd_s.at[ch, 2 + i], dd_r.at[ch, 2 + i], sibling)

    def s4(ch):
        for h in range(2):
            other = (z2, x2)[h]
            for s in range(2):
                i = h * 2 + s
                arrived(
                    line_half(ch, h, other, s),
                    b2_s.at[ch, i],
                    b2_r.at[ch, i],
                    (dev_z, dev_x)[h][s],
                )
            ref = line(ch, h, other)
            send(ref, ref, dd_s.at[ch, 6 + h], dd_r.at[ch, 6 + h], sibling)

    def s5(ch):
        for i in range(8):
            ref = line(ch, (0, 1, 0, 0, 1, 1, 0, 1)[i], z if (0, 1, 0, 0, 1, 1, 0, 1)[i] == 0 else x)
            arrived(ref, dd_s.at[ch, i], dd_r.at[ch, i], sibling)

    plane = [(i, j, k) for i in range(NX) for j in range(NCORE) for k in range(NZ)]

    def h_local():
        return pltpu.make_async_copy(hs_hbm.at[xh, slot], hbuf.at[x, c, z], loc.at[N_CHUNK])

    def h_send():
        h_local().start()
        for n, (i, j, k) in enumerate(plane):
            if n == 0:
                continue
            tx, tc, tz = up(x, i, NX), up(c, j, NCORE), up(z, k, NZ)
            t_slot = tz * 4 + lax.rem(tx, NXL) * 2 + tc
            send(
                hs_hbm.at[tx // NXL, t_slot],
                hbuf.at[x, c, z],
                h_s.at[n],
                h_r.at[n],
                {"xh": tx // NXL, "xl": lax.rem(tx, NXL), "z": tz, "c": tc},
            )

    def h_build():
        h_local().wait()
        for n in range(1, len(plane)):
            arrived(hbuf.at[x, c, z], h_s.at[n], h_r.at[n], sibling)
        for k in range(NY):
            yb = up(y, k, NY)
            for i in range(NX):
                blk = hbuf[i, :, :, :, pl.ds(pl.multiple_of(yb * frows, frows), frows)]
                n_tok = NCORE * NZ * tok
                ht[pl.ds(k * frows, frows), pl.ds(i * n_tok, n_tok)] = blk.reshape(n_tok, frows).T

    def w_copy(ch):
        return pltpu.make_async_copy(
            w_hbm.at[:, pl.ds(ch * chunk, chunk)], wbuf.at[ch % 2], w_sem.at[ch % 2]
        )

    def mm1(ch):
        def body(n, carry):
            col = pl.ds(pl.multiple_of(n * 256, 256), 256)
            g = gbuf[ch, :, :, :, :, col].reshape(NX * NCORE * NZ * tok, 256)
            r = jnp.dot(ht[...], g, preferred_element_type=F32)
            own[ch, :, col] = r[0:frows]
            for k in range(1, NY):
                part[ch, k, :, col] = r[k * frows : (k + 1) * frows].astype(BF)
            return carry

        lax.fori_loop(0, chunk // 256, body, 0)

    def mm2(ch):
        w_copy(ch).wait()

        def body(n, carry):
            row = pl.ds(pl.multiple_of(n * 256, 256), 256)
            g = gbuf[ch, pl.ds(xh * NXL, NXL)].reshape(NXL * NCORE * NZ * tok, chunk)
            r = lax.dot_general(
                g, wbuf[ch % 2, row, :], (((1,), (1,)), ((), ())), preferred_element_type=F32
            )
            if ch == 0:
                acch[:, row] = r
            else:
                acch[:, row] = acch[:, row] + r
            return carry

        lax.fori_loop(0, hid // 256, body, 0)
        if ch + 2 < N_CHUNK:
            w_copy(ch + 2).start()

    row_a, row_b = pl.ds(0, hrow), pl.ds(hrow, hrow)

    def r0(ch):
        send(part.at[ch, 2, row_b], relay.at[ch, 0], rs_s.at[ch, 0], rs_r.at[ch, 0], dev_y[0])
        send(part.at[ch, 2, row_a], relay.at[ch, 1], rs_s.at[ch, 1], rs_r.at[ch, 1], dev_y[1])
        send(part.at[ch, 1, row_a], recv_m.at[ch, row_a], rs_s.at[ch, 2], rs_r.at[ch, 2], dev_y[0])
        send(part.at[ch, 3, row_b], recv_p.at[ch, row_b], rs_s.at[ch, 3], rs_r.at[ch, 3], dev_y[1])

    def r1(ch):
        arrived(relay.at[ch, 0], rs_s.at[ch, 0], rs_r.at[ch, 0], dev_y[0])
        part[ch, 1, row_b] = (part[ch, 1, row_b].astype(F32) + relay[ch, 0].astype(F32)).astype(BF)
        send(part.at[ch, 1, row_b], recv_m.at[ch, row_b], rs_s.at[ch, 4], rs_r.at[ch, 4], dev_y[0])
        arrived(relay.at[ch, 1], rs_s.at[ch, 1], rs_r.at[ch, 1], dev_y[1])
        part[ch, 3, row_a] = (part[ch, 3, row_a].astype(F32) + relay[ch, 1].astype(F32)).astype(BF)
        send(part.at[ch, 3, row_a], recv_p.at[ch, row_a], rs_s.at[ch, 5], rs_r.at[ch, 5], dev_y[1])

    def out_copy(ch):
        return pltpu.make_async_copy(
            own.at[ch], eg_out.at[:, pl.ds(ch * chunk, chunk)], o_sem.at[ch]
        )

    def r2(ch):
        for i in range(2, 6):
            arrived(relay.at[ch, 0], rs_s.at[ch, i], rs_r.at[ch, i], dev_y[i % 2])
        own[ch] = own[ch] + (recv_m[ch].astype(F32) + recv_p[ch].astype(F32))
        out_copy(ch).start()

    group = [(i, j, k) for i in range(NXL) for j in range(NCORE) for k in range(NZ)]

    def hr_send():
        hret[...] = acch[...].astype(BF).reshape(hret.shape)
        for n, (i, j, k) in enumerate(group):
            if n == 0:
                continue
            tx, tc, tz = up(xl, i, NXL), up(c, j, NCORE), up(z, k, NZ)
            send(
                hret.at[tx, tc, tz],
                rbuf.at[slot],
                hr_s.at[n],
                hr_r.at[n],
                {"xl": tx, "z": tz, "c": tc},
            )
        rbuf[slot] = hret[xl, c, z]

    def r_copy():
        return pltpu.make_async_copy(rbuf, r_out, o_sem.at[N_CHUNK])

    def hr_wait():
        for n in range(1, len(group)):
            arrived(rbuf.at[slot], hr_s.at[n], hr_r.at[n], sibling)
        r_copy().start()

    owners = [(i, j) for i in range(NY) for j in range(NXH)]

    def d_local():
        return (
            pltpu.make_async_copy(
                x_hbm.at[:, pl.ds(pl.multiple_of(dp * dcols, 128), dcols)],
                xbuf.at[dp],
                loc.at[N_CHUNK + 1],
            ),
            pltpu.make_async_copy(lat_hbm, lbuf.at[dp], loc.at[N_CHUNK + 2]),
        )

    def d0():
        for d in d_local():
            d.start()
        for n, (i, j) in enumerate(owners):
            if n == 0:
                continue
            ty, th = up(y, i, NY), up(xh, j, NXH)
            td = ty * 2 + th
            dev = {"y": ty, "xh": th}
            send(
                x_hbm.at[:, pl.ds(pl.multiple_of(td * dcols, 128), dcols)],
                xbuf.at[dp],
                dx_s.at[n],
                dx_r.at[n],
                dev,
            )
            send(lat_hbm, lbuf.at[dp], dl_s.at[n], dl_r.at[n], dev)

    def d1():
        for d in d_local():
            d.wait()
        for n in range(1, len(owners)):
            arrived(xbuf.at[dp], dx_s.at[n], dx_r.at[n], sibling)
            arrived(lbuf.at[dp], dl_s.at[n], dl_r.at[n], sibling)
        n_tok = len(owners) * tok

        def body(n, carry):
            col = pl.ds(pl.multiple_of(n * 128, 128), 128)
            xt = xbuf[:, :, col].reshape(n_tok, 128).T
            dpart[col, :] = jnp.dot(
                xt, lbuf[...].reshape(n_tok, lbuf.shape[-1]), preferred_element_type=F32
            )
            return carry

        lax.fori_loop(0, dcols // 128, body, 0)
        for n, (i, j, k) in enumerate(group):
            if n == 0:
                continue
            tx, tc, tz = up(xl, i, NXL), up(c, j, NCORE), up(z, k, NZ)
            ts = tz * 4 + tx * 2 + tc
            send(
                dpart.at[pl.ds(pl.multiple_of(ts * drows, 8), drows)],
                drecv.at[slot],
                ds_s.at[n],
                ds_r.at[n],
                {"xl": tx, "z": tz, "c": tc},
            )
        drecv[slot] = dpart[pl.ds(pl.multiple_of(slot * drows, 8), drows)]

    def d2():
        for n in range(1, len(group)):
            arrived(drecv.at[slot], ds_s.at[n], ds_r.at[n], sibling)
        total = drecv[0]
        for n in range(1, len(group)):
            total = total + drecv[n]
        dg_out[...] = total

    w_copy(0).start()
    w_copy(1).start()
    s0(0)
    d0()
    s0(1)
    s1(0)
    s2(0)
    h_send()
    s1(1)
    s3(0)
    s2(1)
    s0(2)
    s0(3)
    s4(0)
    s3(1)
    h_build()
    s1(2)
    s2(2)
    s5(0)
    mm1(0)
    r0(0)
    s4(1)
    s3(2)
    s1(3)
    s2(3)
    mm2(0)
    s5(1)
    mm1(1)
    r0(1)
    s4(2)
    s3(3)
    r1(0)
    mm2(1)
    s5(2)
    mm1(2)
    r0(2)
    s4(3)
    d1()
    r1(1)
    mm2(2)
    s5(3)
    mm1(3)
    r0(3)
    mm2(3)
    hr_send()
    r2(0)
    r1(2)
    r2(1)
    d2()
    hr_wait()
    r1(3)
    r2(2)
    r2(3)
    for ch in range(N_CHUNK):
        out_copy(ch).wait()
    r_copy().wait()
    for d in sent:
        d.wait_send()


def exchange(g, hs, w, xin, lat):
    tok, d = g.shape
    chunk = d // N_CHUNK
    hid = w.shape[0]
    n_plane = NX * NCORE * NZ
    frows = hid // NXH // NY
    kvr = lat.shape[1]
    drows = d // 128
    dma = pltpu.SemaphoreType.DMA
    any_spec = pl.BlockSpec(memory_space=pl.ANY)
    v = pltpu.VMEM
    scratch = [
        v((N_CHUNK, NX, NCORE, NZ, tok, chunk), BF),
        v((NX, NCORE, NZ, tok, hid // NXH), BF),
        v((hid // NXH, n_plane * tok), BF),
        v((2, hid, chunk), BF),
        v((16 * tok, hid), F32),
        v((NXL, NCORE, NZ, tok, hid), BF),
        v((16, tok, hid), BF),
        v((N_CHUNK, NY, frows, chunk), BF),
        v((N_CHUNK, frows, chunk), F32),
        v((N_CHUNK, 2, frows // 2, chunk), BF),
        v((N_CHUNK, frows, chunk), BF),
        v((N_CHUNK, frows, chunk), BF),
        v((8, tok, d // 8), BF),
        v((8, tok, kvr), BF),
        v((d // 8, kvr), F32),
        v((16, drows, kvr), F32),
    ]
    sems = []
    for shape in ((N_CHUNK, 4), (N_CHUNK, 4), (N_CHUNK, 4), (N_CHUNK, 4), (N_CHUNK, 8), (32,), (N_CHUNK, 6), (16,), (8,), (8,), (16,)):
        sems += [dma(shape), dma(shape)]
    sems += [dma((N_CHUNK + 3,)), dma((2,)), dma((N_CHUNK + 1,))]
    return pl.pallas_call(
        kernel,
        out_shape=(
            jax.ShapeDtypeStruct((16, tok, hid), BF),
            jax.ShapeDtypeStruct((frows, d), F32),
            jax.ShapeDtypeStruct((drows, kvr), F32),
        ),
        in_specs=[any_spec] * 5,
        out_specs=(any_spec, any_spec, pl.BlockSpec(memory_space=pltpu.VMEM)),
        scratch_shapes=scratch + sems,
        compiler_params=pltpu.CompilerParams(
            has_side_effects=True, vmem_limit_bytes=62 * 1024 * 1024
        ),
        name="exchange",
    )(g, hs, w, xin, lat)


def on_device(
    expert_ids,
    expert_home,
    live_tokens,
    gate_weights,
    output_grad,
    saved_hidden,
    down_weight,
    dense_input,
    latent_grad,
):
    tok, topk = expert_ids.shape
    hid = saved_hidden.shape[2]
    n_slot = 16
    is_live = jnp.arange(tok, dtype=jnp.int32) < live_tokens[0]
    masked = jnp.where(is_live[:, None], latent_grad, jnp.zeros_like(latent_grad))
    ids = expert_ids.reshape(tok * topk)
    table = ids[:, None] == jnp.arange(n_slot, dtype=jnp.int32)[None, :]
    home = jnp.sum(jnp.where(table, expert_home[None, :], 0), axis=1)
    token = jnp.arange(tok * topk, dtype=jnp.int32) // topk
    place = home * tok + token
    pick = (jnp.arange(n_slot * tok, dtype=jnp.int32)[:, None] == place[None, :]).astype(BF)
    scale = (gate_weights * is_live[:, None].astype(F32)).reshape(tok * topk)
    scaled = (saved_hidden.reshape(tok * topk, hid).astype(F32) * scale[:, None]).astype(BF)
    halves = scaled.reshape(tok * topk, NY, NXH, hid // 8)
    hs = jnp.stack(
        [
            jnp.dot(
                pick,
                halves[:, :, j].reshape(tok * topk, hid // 2),
                preferred_element_type=F32,
            ).astype(BF)
            for j in range(NXH)
        ]
    ).reshape(NXH, n_slot, tok, hid // 2)
    r, eg, dg = exchange(output_grad, hs, down_weight[0], dense_input, masked)
    back = lax.dot_general(
        pick, r.reshape(n_slot * tok, hid), (((0,), (0,)), ((), ())), preferred_element_type=F32
    )
    hg = (back * scale[:, None]).astype(BF).reshape(tok, topk, hid)
    return hg, eg[None], dg


def solution(mesh):
    torus = Mesh(mesh.devices.reshape(4, 2, 4, 2, 2), ALL)
    in_specs = (
        P(ALL, None),
        P(),
        P(ALL),
        P(ALL, None),
        P(ALL, None),
        P(ALL, None, None),
        P(EXPERT, None, None),
        P(ALL, None),
        P(ALL, None),
    )
    out_specs = (P(ALL, None, None), P(EXPERT, DP, None), P(ALL, None))
    return jax.shard_map(
        on_device, mesh=torus, in_specs=in_specs, out_specs=out_specs, check_vma=False
    )
```

time: 504 us -> 148 us (0.29)
  waiting for transfers between devices: 364 us -> 0 us
  Pallas kernels: 0 us -> 130 us
  local copies, waits for them, and re-layouts: 51.8 us -> 9.63 us
  matrix products: 30 us -> 3.18 us
  starting transfers between devices: 20.3 us -> 0 us
  between operations: 16.4 us -> 1.35 us
  blocking collectives: 8.37 us -> 0 us
  other arithmetic: 11.3 us -> 4.36 us
    all_gather x1 -> x0, waiting for transfers between devices: 275 us -> none  [on_device(): lax.all_gather(masked_grad, DP_EXPERT, axis=0, tiled=True)]
    pallas_call x0 -> x1, Pallas kernels: none -> 130 us  [exchange(): pl.pallas_call(kernel, out_shape=(jax.ShapeDtypeStruct((16, tok, hid), BF...]
    all_to_all x3 -> x0, waiting for transfers between devices: 89.1 us -> none  [the longest x1 73.3 us: side_by_side(): lax.all_to_all(both, axis, split_axis=split_dim, concat_axis=concat_dim,...]
    dot_general x3, matrix products: 30 us -> 3.18 us  [the longest x1 2.51 us: on_device(): lax.dot_general(pick, r.reshape(n_slot * tok, hid), (((0,), (0,)), ((), (...]
    all_to_all x3 -> x0, starting transfers between devices: 20 us -> none  [the longest x2 13.4 us: moved_by_axis(): result = lax.all_to_all(result, axes[k], k, k, tiled=True)]
    gather x5 -> x0, local copies, waits for them, and re-layouts: 12.8 us -> none  [the longest x1 6.14 us: on_device(): output_grad[source_token].astype(jnp.float32) * slot_scale[:, None]]
    reshape x4 -> x0, local copies, waits for them, and re-layouts: 10.4 us -> none  [the longest x1 7.34 us: on_device(): arrived_grad = arrived_grad.reshape(n_group * capacity, model_width)]
    all_to_all x2 -> x0, blocking collectives: 8.37 us -> none  [moved_by_axis(): result = lax.all_to_all(result, axes[k], k, k, tiled=True)]
  transfers between devices with their start and end apart: 5 -> 0, of which waited for: 3 -> 0; matrix products, arithmetic and copies ran while one was open for 12% -> 0% of each run, Pallas kernels for 0% -> 0%
where the time goes in v1:
time: 148 us
  Pallas kernels  130 us (88%)
  local copies, waits for them, and re-layouts  9.63 us (7%)
  other arithmetic  4.36 us (3%)
  matrix products  3.18 us (2%)
    pallas_call x1, Pallas kernels, exchange(): pl.pallas_call(kernel, out_shape=(jax.ShapeDtypeStruct((16, tok, hid), BF...  130 us
    unnamed x5, local copies, waits for them, and re-layouts  5.62 us

profile of v1, /device:TPU:0, one launch (start us, length us, event | category | flops | bytes accessed | tf_op | source)
XLA Modules:
  0.0 148.1 jit_solution(13213369140459455828)
XLA Ops:
  1.3 0.7 broadcast_multiply_fusion
  2.0 0.1 copy.19
  2.1 0.1 mul.41
  2.1 1.4 broadcast_select_fusion.lat_hbm
  3.6 0.8 copy.18
  4.3 0.1 eq.29
  4.4 0.7 select_reduce_fusion
  5.2 2.1 %reshape.57 = f32[256,4,2,128]{3,2,1,0:T(2,128)S(1)} reshape(bf16[32,8,1024]{2,1,0:T(8,128)(2,1)} %param.14) | data formatting | bytes 1572864 | tf_op jit(solution)/shard_map/convert_element_type | solution.py:530
  7.2 0.4 multiply_convert_fusion
  7.7 0.7 fusion.7
  8.4 0.5 copy.20
  8.9 0.3 convolution_convert_fusion.1
  9.3 0.5 copy.21
  9.7 0.3 convolution_convert_fusion
  10.1 1.1 pad_maximum_fusion.hs_hbm
  11.1 129.6 %exchange.1 = (bf16[16,32,1024]{2,1,0:T(8,128)(2,1)}, f32[128,7168]{1,0:T(8,128)}, f32[56,256]{1,0:T(8,128)}) custom-call(bf16[32,7168]{1,0:T(8,128)(2,1)} %g_hbm.1, bf16[2,16,32,512]{3,2,1,0:T(8,128)(2,1)} %pad_maximum_fusion.hs_hbm, bf16[1024,7168]{1,0:T(8,128)(2,1)} %bitcast.14, bf16[32,7168]{1,0:T(8,128)(2,1)} %x_hbm.1, ...), custom_call_target="tpu_custom_call" | custom-call | tf_op jit(solution)/shard_map/exchange/pallas_call | solution.py:490
  140.8 2.5 %fusion.1 = bf16[32,8,1024]{2,1,0:T(8,128)(2,1)} fusion(bf16[512,1024]{1,0:T(8,128)(2,1)} %bitcast.20, f32[256]{0:T(256)S(1)} %mul.41, s32[256]{0:T(256)S(1)} %fusion.5), kind=kOutput, calls=%fused_computation.4 | convolution fusion | flops 269090816 | bytes 1574912 | tf_op jit(solution)/shard_map/dot_general | solution.py:543
  143.3 0.0 copy-start
  143.3 4.2 %copy.25 = f32[1,128,7168]{2,1,0:T(8,128)} copy(f32[1,128,7168]{2,1,0:T(8,128)} %bitcast.15) | data formatting | bytes 7340032
  147.5 0.0 copy-done
  147.5 0.6 copy.26
  (2 shorter events, 0.0 us)
Async XLA Ops:
  143.3 4.2 %copy-start = (f32[56,256]{1,0:T(8,128)S(1)}, f32[56,256]{1,0:T(8,128)}, u32[]{:S(2)}) copy-start(f32[56,256]{1,0:T(8,128)} %get-tuple-element.18) | copy-start | bytes 172036

commit v2 on v0

v2 whole, which is shorter than its diff:
```python
import jax
import jax.numpy as jnp
from jax import lax
from jax.experimental import pallas as pl
from jax.experimental.pallas import tpu as pltpu
from jax.sharding import Mesh
from jax.sharding import PartitionSpec as P

DP = ("y", "xh")
EXPERT = ("z", "xl", "c")
ALL = ("y", "xh", "z", "xl", "c")
MESH = pl.DeviceIdType.MESH
NY, NX, NZ, NCORE, NXH, NXL = 4, 4, 4, 2, 2, 2
N_SLOT = 16
BF = jnp.bfloat16
F32 = jnp.float32
WIDTHS = (768, 1280, 1536, 1792, 1792)
N_CHUNK = len(WIDTHS)
STARTS = tuple(sum(WIDTHS[:i]) for i in range(N_CHUNK))
PLANE = [(i, j, k) for i in range(NX) for j in range(NCORE) for k in range(NZ)]
GROUP = [(i, j, k) for i in range(NXL) for j in range(NCORE) for k in range(NZ)]
OWNERS = [(i, j) for i in range(NY) for j in range(NXH)]


def up(v, k, n):
    return lax.rem(v + k, n)


def kernel(names, *all_refs):
    r = dict(zip(names, all_refs))
    ids, home, live, gates, lat = (r[k] for k in ("ids", "home", "live", "gates", "lat"))
    g_hbm, sv_hbm, w_hbm, x_hbm = (r[k] for k in ("g", "sv", "w", "x"))
    hg_out, eg_out, dg_out = r["hg_out"], r["eg_out"], r["dg_out"]
    gbuf, part, relay, recv_p, recv_m = (
        [r[k + str(i)] for i in range(N_CHUNK)] for k in ("gbuf", "part", "relay", "recv_p", "recv_m")
    )
    hs, hbuf, ht, wbuf, acch, hret, rbuf = (
        r[k] for k in ("hs", "hbuf", "ht", "wbuf", "acch", "hret", "rbuf")
    )
    saved, pick, pick_t, coef, flip = (r[k] for k in ("saved", "pick", "pick_t", "coef", "flip"))
    xbuf, lsend, lbuf, dpart, dsend, drecv = (
        r[k] for k in ("xbuf", "lsend", "lbuf", "dpart", "dsend", "drecv")
    )

    y = lax.axis_index("y")
    xh = lax.axis_index("xh")
    z = lax.axis_index("z")
    xl = lax.axis_index("xl")
    c = lax.axis_index("c")
    x = xh * NXL + xl
    slot = z * 4 + xl * 2 + c
    dp = y * 2 + xh
    tok = g_hbm.shape[0]
    half_tok = tok // 2
    topk = ids.shape[0]
    pairs = tok * topk
    frows = ht.shape[0] // NY
    hrow = frows // 2
    hid = w_hbm.shape[0]
    dcols = xbuf.shape[-1]
    drows = drecv.shape[1]
    rows_of = (pl.ds(0, half_tok), pl.ds(half_tok, half_tok))

    def at_x(v):
        return {"xh": v // NXL, "xl": lax.rem(v, NXL)}

    xp, xm, x2 = up(x, 1, NX), up(x, NX - 1, NX), up(x, 2, NX)
    zp, zm, z2 = up(z, 1, NZ), up(z, NZ - 1, NZ), up(z, 2, NZ)
    yp, ym = up(y, 1, NY), up(y, NY - 1, NY)
    dev_x = (at_x(xp), at_x(xm), at_x(x2))
    dev_z = ({"z": zp}, {"z": zm}, {"z": z2})
    dev_y = ({"y": yp}, {"y": ym})
    sibling = {"c": 1 - c}
    sent = []

    def sems(name, *at):
        return r[name + "_s"].at[at], r[name + "_r"].at[at]

    def remote(src, dst, pair, dev):
        return pltpu.make_async_remote_copy(
            src_ref=src,
            dst_ref=dst,
            send_sem=pair[0],
            recv_sem=pair[1],
            device_id=dev,
            device_id_type=MESH,
        )

    def send(src, dst, pair, dev):
        d = remote(src, dst, pair, dev)
        d.start()
        sent.append(d)

    def arrived(ref, pair, dev):
        remote(ref, ref, pair, dev).wait_recv()

    def plane_dev(n):
        i, j, k = PLANE[n]
        tx, tc, tz = up(x, i, NX), up(c, j, NCORE), up(z, k, NZ)
        return tx, tc, tz, {"xh": tx // NXL, "xl": lax.rem(tx, NXL), "z": tz, "c": tc}

    barrier = pltpu.get_barrier_semaphore()

    def greet():
        for n in range(1, len(PLANE)):
            pl.semaphore_signal(barrier, inc=1, device_id=plane_dev(n)[3], device_id_type=MESH)
        for i, j in OWNERS:
            if i:
                dev = {"y": up(y, i, NY), "xh": up(xh, j, NXH)}
                pl.semaphore_signal(barrier, inc=1, device_id=dev, device_id_type=MESH)

    def bar():
        pl.semaphore_wait(barrier, len(PLANE) - 1 + 2 * (NY - 1))

    def own_copy(ch):
        return pltpu.make_async_copy(
            g_hbm.at[:, pl.ds(STARTS[ch], WIDTHS[ch])], gbuf[ch].at[x, c, z], r["loc"].at[ch]
        )

    def saved_copy():
        return pltpu.make_async_copy(sv_hbm, saved, r["loc"].at[N_CHUNK])

    def h_local():
        return pltpu.make_async_copy(hs.at[xh, slot], hbuf.at[x, c, z], r["loc"].at[N_CHUNK + 1])

    def d_local():
        return pltpu.make_async_copy(
            x_hbm.at[:, pl.ds(pl.multiple_of(dp * dcols, 128), dcols)],
            xbuf.at[dp],
            r["loc"].at[N_CHUNK + 2],
        )

    def w_copy(ch):
        return pltpu.make_async_copy(
            w_hbm.at[:, pl.ds(STARTS[ch], WIDTHS[ch])],
            wbuf.at[ch % 2, :, pl.ds(0, WIDTHS[ch])],
            r["w_sem"].at[ch % 2],
        )

    def prep():
        homes = jnp.zeros(ids.shape, F32)
        for e in range(N_SLOT):
            homes = jnp.where(ids[...] == e, home[e].astype(F32), homes)
        is_live = lax.broadcasted_iota(jnp.int32, ids.shape, 1) < live[0]
        flip[...] = jnp.zeros_like(flip)
        flip[0, 0:topk, 0:tok] = homes
        flip[1, 0:topk, 0:tok] = jnp.where(is_live, gates[...], jnp.zeros_like(gates))
        home_t = flip[0].T[0:tok]
        scale_t = flip[1].T[0:tok]
        lane = lax.broadcasted_iota(jnp.int32, (128, pairs), 1)
        row = lax.broadcasted_iota(jnp.int32, (128, pairs), 0)
        spread = jnp.where(lax.rem(lane, topk) == row, 1.0, 0.0).astype(BF)
        wide = jnp.dot(home_t.astype(BF), spread, preferred_element_type=F32)
        lane = lax.broadcasted_iota(jnp.int32, (tok, pairs), 1)
        row = lax.broadcasted_iota(jnp.int32, (tok, pairs), 0)
        wide = jnp.where(lane // topk == row, wide, -1.0)
        column = lax.broadcasted_iota(jnp.int32, (tok, 128), 1)
        for s in range(N_SLOT):
            pick[s] = jnp.where(wide == float(s), 1.0, 0.0).astype(BF)
            mine = jnp.where((home_t == float(s)) & (column < topk), scale_t, 0.0)
            coef[s] = jnp.broadcast_to(jnp.sum(mine, axis=1, keepdims=True), (tok, 128))
        token = lax.broadcasted_iota(jnp.int32, lat.shape, 0)
        lsend[...] = jnp.where(token < live[0], lat[...], jnp.zeros_like(lat))
        saved_copy().wait()
        table = pick[...].reshape(N_SLOT * tok, pairs)
        scale = coef[...].reshape(N_SLOT * tok, 128)
        for n in range(NY):
            rows = jnp.dot(table, saved[:, n * 256 : (n + 1) * 256], preferred_element_type=F32)
            for j in range(NXH):
                scaled = (rows[:, j * frows : (j + 1) * frows] * scale).astype(BF)
                hs[j, :, :, n * frows : (n + 1) * frows] = scaled.reshape(N_SLOT, tok, frows)

    def lanes(ch, h):
        return pl.ds(h * (WIDTHS[ch] // 2), WIDTHS[ch] // 2)

    def direct(ch):
        return ch == 0

    def s0(ch):
        own_copy(ch).wait()
        for h in range(2):
            ref = gbuf[ch].at[x, c, z, :, lanes(ch, h)]
            for s in range(3 if direct(ch) else 2):
                send(ref, ref, sems("a1", ch, h * 3 + s), (dev_x, dev_z)[h][s])

    def s1(ch):
        for h in range(2):
            for s in range(2):
                if h == 0:
                    blk = gbuf[ch].at[(xm, xp)[s], c, z]
                else:
                    blk = gbuf[ch].at[x, c, (zm, zp)[s]]
                dev = (dev_x, dev_z)[h][s]
                arrived(blk.at[:, lanes(ch, h)], sems("a1", ch, h * 3 + s), dev)
                ref = blk.at[rows_of[s], lanes(ch, h)]
                send(ref, ref, sems("a2", ch, h * 2 + s), dev)

    def line(ch, h, other):
        if h == 0:
            return gbuf[ch].at[:, c, other, :, lanes(ch, 0)]
        return gbuf[ch].at[other, c, :, :, lanes(ch, 1)]

    def line_half(ch, h, other, s):
        if h == 0:
            return gbuf[ch].at[:, c, other, rows_of[s], lanes(ch, 0)]
        return gbuf[ch].at[other, c, :, rows_of[s], lanes(ch, 1)]

    def s2(ch):
        for h in range(2):
            dev = (dev_x, dev_z)[h]
            blk = gbuf[ch].at[x2, c, z] if h == 0 else gbuf[ch].at[x, c, z2]
            if direct(ch):
                for s in range(3):
                    arrived(blk.at[:, lanes(ch, h)], sems("a1", ch, h * 3 + s), dev[s])
            else:
                for s in range(2):
                    arrived(blk.at[rows_of[s], lanes(ch, h)], sems("a2", ch, h * 2 + s), dev[s])
            ref = line(ch, h, (z, x)[h])
            for s in range(2):
                send(ref, ref, sems("b1", ch, h * 2 + s), (dev_z, dev_x)[h][s])
            send(ref, ref, sems("dd", ch, h), sibling)

    def s3(ch):
        for h in range(2):
            for s in range(2):
                i = h * 2 + s
                other = ((zm, zp), (xm, xp))[h][s]
                dev = (dev_z, dev_x)[h][s]
                ref = line(ch, h, other)
                arrived(ref, sems("b1", ch, i), dev)
                fwd = line_half(ch, h, other, s)
                send(fwd, fwd, sems("b2", ch, i), dev)
                send(ref, ref, sems("dd", ch, 2 + i), sibling)

    def s4(ch):
        for h in range(2):
            other = (z2, x2)[h]
            for s in range(2):
                dev = (dev_z, dev_x)[h][s]
                arrived(line_half(ch, h, other, s), sems("b2", ch, h * 2 + s), dev)
            ref = line(ch, h, other)
            send(ref, ref, sems("dd", ch, 6 + h), sibling)

    def s5(ch):
        for i, h in enumerate((0, 1, 0, 0, 1, 1, 0, 1)):
            arrived(line(ch, h, (z, x)[h]), sems("dd", ch, i), sibling)

    def h_send(first, last):
        if first == 0:
            h_local().start()
        for m in range(first, last):
            n = ((m + 1) * 11) % len(PLANE)
            tx, tc, tz, dev = plane_dev(n)
            t_slot = tz * 4 + lax.rem(tx, NXL) * 2 + tc
            send(hs.at[tx // NXL, t_slot], hbuf.at[x, c, z], sems("h", n), dev)

    def h_build():
        h_local().wait()
        for n in range(1, len(PLANE)):
            arrived(hbuf.at[x, c, z], sems("h", n), sibling)
        n_tok = NCORE * NZ * tok
        for k in range(NY):
            col = pl.ds(pl.multiple_of(up(y, k, NY) * frows, frows), frows)
            for i in range(NX):
                blk = hbuf[i, :, :, :, col].reshape(n_tok, frows)
                ht[pl.ds(k * frows, frows), pl.ds(i * n_tok, n_tok)] = blk.T

    def mm1(ch):
        def body(n, carry):
            col = pl.ds(pl.multiple_of(n * 256, 256), 256)
            g = gbuf[ch][:, :, :, :, col].reshape(len(PLANE) * tok, 256)
            p = jnp.dot(ht[...], g, preferred_element_type=F32)
            eg_out[:, pl.ds(pl.multiple_of(STARTS[ch] + n * 256, 256), 256)] = p[0:frows]
            for k in range(1, NY):
                part[ch][k - 1, :, col] = p[k * frows : (k + 1) * frows].astype(BF)
            return carry

        lax.fori_loop(0, WIDTHS[ch] // 256, body, 0)

    def mm2(ch):
        w_copy(ch).wait()

        def body(n, carry):
            row = pl.ds(pl.multiple_of(n * 256, 256), 256)
            g = gbuf[ch][pl.ds(xh * NXL, NXL)].reshape(len(GROUP) * tok, WIDTHS[ch])
            w = wbuf[ch % 2, row, pl.ds(0, WIDTHS[ch])]
            p = lax.dot_general(g, w, (((1,), (1,)), ((), ())), preferred_element_type=F32)
            if ch == 0:
                acch[:, row] = p
            else:
                acch[:, row] = acch[:, row] + p
            return carry

        lax.fori_loop(0, hid // 256, body, 0)
        if ch + 2 < N_CHUNK:
            w_copy(ch + 2).start()

    row_a, row_b = pl.ds(0, hrow), pl.ds(hrow, hrow)

    def r0(ch):
        p = part[ch]
        send(p.at[1, row_b], relay[ch].at[0], sems("rs", ch, 0), dev_y[0])
        send(p.at[1, row_a], relay[ch].at[1], sems("rs", ch, 1), dev_y[1])
        send(p.at[0, row_a], recv_m[ch].at[row_a], sems("rs", ch, 2), dev_y[0])
        send(p.at[2, row_b], recv_p[ch].at[row_b], sems("rs", ch, 3), dev_y[1])

    def r1(ch):
        p = part[ch]
        arrived(relay[ch].at[0], sems("rs", ch, 0), dev_y[0])
        p[0, row_b] = (p[0, row_b].astype(F32) + relay[ch][0].astype(F32)).astype(BF)
        send(p.at[0, row_b], recv_m[ch].at[row_b], sems("rs", ch, 4), dev_y[0])
        arrived(relay[ch].at[1], sems("rs", ch, 1), dev_y[1])
        p[2, row_a] = (p[2, row_a].astype(F32) + relay[ch][1].astype(F32)).astype(BF)
        send(p.at[2, row_a], recv_p[ch].at[row_a], sems("rs", ch, 5), dev_y[1])

    def r2(ch):
        for i in range(2, 6):
            arrived(relay[ch].at[0], sems("rs", ch, i), dev_y[i % 2])
        col = pl.ds(STARTS[ch], WIDTHS[ch])
        eg_out[:, col] = eg_out[:, col] + (recv_m[ch][...].astype(F32) + recv_p[ch][...].astype(F32))

    def group_dev(n):
        i, j, k = GROUP[n]
        tx, tc, tz = up(xl, i, NXL), up(c, j, NCORE), up(z, k, NZ)
        return tx, tc, tz, {"xl": tx, "z": tz, "c": tc}

    def hr_send():
        hret[...] = acch[...].astype(BF).reshape(hret.shape)
        for n in range(1, len(GROUP)):
            tx, tc, tz, dev = group_dev(n)
            send(hret.at[tx, tc, tz], rbuf.at[slot], sems("hr", n), dev)
        rbuf[slot] = hret[xl, c, z]

    def table_flip():
        pick_t[...] = pick[...].reshape(N_SLOT * tok, pairs).T

    def hr_wait():
        for n in range(1, len(GROUP)):
            arrived(rbuf.at[slot], sems("hr", n), sibling)
        scale = coef[...].reshape(N_SLOT * tok, 128)
        for n in range(hid // 256):
            halves = []
            for j in range(2):
                rows = rbuf[:, :, n * 256 + j * 128 : n * 256 + (j + 1) * 128]
                rows = rows.reshape(N_SLOT * tok, 128).astype(F32) * scale
                halves.append(rows.astype(BF))
            rows = jnp.concatenate(halves, axis=1)
            back = jnp.dot(pick_t[...], rows, preferred_element_type=F32)
            hg_out[:, n * 256 : (n + 1) * 256] = back.astype(BF)

    def d0(both):
        if not both:
            d_local().start()
            lbuf[dp] = lsend[...]
        for n, (i, j) in enumerate(OWNERS):
            if n == 0 or j != both:
                continue
            ty, th = up(y, i, NY), up(xh, j, NXH)
            td = ty * 2 + th
            dev = {"y": ty, "xh": th}
            send(
                x_hbm.at[:, pl.ds(pl.multiple_of(td * dcols, 128), dcols)],
                xbuf.at[dp],
                sems("dx", n),
                dev,
            )
            send(lsend, lbuf.at[dp], sems("dl", n), dev)

    def d1():
        d_local().wait()
        for n in range(1, len(OWNERS)):
            arrived(xbuf.at[dp], sems("dx", n), sibling)
            arrived(lbuf.at[dp], sems("dl", n), sibling)
        n_tok = len(OWNERS) * tok

        def body(n, carry):
            col = pl.ds(pl.multiple_of(n * 128, 128), 128)
            xt = xbuf[:, :, col].reshape(n_tok, 128).T
            dpart[col, :] = jnp.dot(
                xt, lbuf[...].reshape(n_tok, lbuf.shape[-1]), preferred_element_type=F32
            )
            return carry

        lax.fori_loop(0, dcols // 128, body, 0)
        for n in range(N_SLOT):
            dsend[n] = dpart[n * drows : (n + 1) * drows].astype(BF)
        for n in range(1, len(GROUP)):
            tx, tc, tz, dev = group_dev(n)
            send(dsend.at[tz * 4 + tx * 2 + tc], drecv.at[slot], sems("ds", n), dev)
        drecv[slot] = dsend[slot]

    def d2():
        for n in range(1, len(GROUP)):
            arrived(drecv.at[slot], sems("ds", n), sibling)
        mine = dpart[pl.ds(pl.multiple_of(slot * drows, 8), drows)]
        total = mine - drecv[slot].astype(F32)
        for n in range(len(GROUP)):
            total = total + drecv[n].astype(F32)
        dg_out[...] = total

    greet()
    saved_copy().start()
    own_copy(0).start()
    own_copy(1).start()
    own_copy(2).start()
    own_copy(3).start()
    own_copy(4).start()
    w_copy(0).start()
    w_copy(1).start()
    prep()
    bar()
    s0(0)
    h_send(0, 7)
    s2(0)
    s0(1)
    h_send(7, 15)
    s3(0)
    h_send(15, 31)
    s1(1)
    s4(0)
    s2(1)
    s0(2)
    table_flip()
    h_build()
    s5(0)
    mm1(0)
    r0(0)
    d0(0)
    s0(3)
    s0(4)
    s1(2)
    s3(1)
    s2(2)
    s4(1)
    mm2(0)
    s1(3)
    s5(1)
    mm1(1)
    r0(1)
    s3(2)
    s2(3)
    s1(4)
    s4(2)
    mm2(1)
    r1(0)
    s3(3)
    s2(4)
    s5(2)
    mm1(2)
    r0(2)
    s4(3)
    mm2(2)
    s3(4)
    d0(1)
    s5(3)
    mm1(3)
    r0(3)
    r1(1)
    s4(4)
    mm2(3)
    s5(4)
    mm1(4)
    r0(4)
    mm2(4)
    hr_send()
    r1(2)
    d1()
    r2(0)
    r2(1)
    r1(3)
    r2(2)
    hr_wait()
    r1(4)
    d2()
    r2(3)
    r2(4)
    for d in sent:
        d.wait_send()


def exchange(ids, home, live, gates, lat, g, sv, w, xin):
    tok, d = g.shape
    pairs, hid = sv.shape
    kvr = lat.shape[1]
    frows = hid // 8
    drows = d // 128
    dma = pltpu.SemaphoreType.DMA
    v = pltpu.VMEM
    smem, vmem, hbm = (
        pl.BlockSpec(memory_space=m) for m in (pltpu.SMEM, pltpu.VMEM, pl.ANY)
    )
    ins = {
        "ids": vmem, "home": smem, "live": smem, "gates": vmem, "lat": vmem,
        "g": hbm, "sv": hbm, "w": hbm, "x": hbm,
    }
    outs = ("hg_out", "eg_out", "dg_out")
    scratch = {
        "hs": v((NXH, N_SLOT, tok, hid // NXH), BF),
        "hbuf": v((NX, NCORE, NZ, tok, hid // NXH), BF),
        "ht": v((hid // NXH, len(PLANE) * tok), BF),
        "wbuf": v((2, hid, max(WIDTHS)), BF),
        "acch": v((len(GROUP) * tok, hid), F32),
        "hret": v((NXL, NCORE, NZ, tok, hid), BF),
        "rbuf": v((N_SLOT, tok, hid), BF),
        "saved": v((pairs, hid), BF),
        "pick": v((N_SLOT, tok, pairs), BF),
        "pick_t": v((pairs, N_SLOT * tok), BF),
        "coef": v((N_SLOT, tok, 128), F32),
        "flip": v((2, 128, 128), F32),
        "xbuf": v((8, tok, d // 8), BF),
        "lsend": v((tok, kvr), BF),
        "lbuf": v((8, tok, kvr), BF),
        "dpart": v((d // 8, kvr), F32),
        "dsend": v((N_SLOT, drows, kvr), BF),
        "drecv": v((N_SLOT, drows, kvr), BF),
        "loc": dma((N_CHUNK + 3,)),
        "w_sem": dma((2,)),
    }
    for i, width in enumerate(WIDTHS):
        scratch["gbuf" + str(i)] = v((NX, NCORE, NZ, tok, width), BF)
        scratch["part" + str(i)] = v((NY - 1, frows, width), BF)
        scratch["relay" + str(i)] = v((2, frows // 2, width), BF)
        scratch["recv_p" + str(i)] = v((frows, width), BF)
        scratch["recv_m" + str(i)] = v((frows, width), BF)
    pairs_of = {
        "a1": (N_CHUNK, 6), "a2": (N_CHUNK, 4), "b1": (N_CHUNK, 4), "b2": (N_CHUNK, 4),
        "dd": (N_CHUNK, 8), "h": (32,), "rs": (N_CHUNK, 6), "hr": (16,), "dx": (8,),
        "dl": (8,), "ds": (16,),
    }
    for name, shape in pairs_of.items():
        scratch[name + "_s"] = dma(shape)
        scratch[name + "_r"] = dma(shape)
    names = tuple(ins) + outs + tuple(scratch)

    def body(*refs):
        kernel(names, *refs)

    return pl.pallas_call(
        body,
        out_shape=(
            v((pairs, hid), BF),
            v((frows, d), F32),
            v((drows, kvr), F32),
        ),
        in_specs=list(ins.values()),
        out_specs=(vmem, vmem, vmem),
        scratch_shapes=list(scratch.values()),
        compiler_params=pltpu.CompilerParams(
            collective_id=0, has_side_effects=True, vmem_limit_bytes=56 * 1024 * 1024
        ),
        name="exchange",
    )(ids, home, live, gates, lat, g, sv, w, xin)


def on_device(
    expert_ids,
    expert_home,
    live_tokens,
    gate_weights,
    output_grad,
    saved_hidden,
    down_weight,
    dense_input,
    latent_grad,
):
    tok, topk = expert_ids.shape
    hid = saved_hidden.shape[2]
    hg, eg, dg = exchange(
        expert_ids.T,
        expert_home,
        live_tokens,
        gate_weights.T,
        latent_grad,
        output_grad,
        saved_hidden.reshape(tok * topk, hid),
        down_weight[0],
        dense_input,
    )
    return hg.reshape(tok, topk, hid), eg[None], dg


def solution(mesh):
    torus = Mesh(mesh.devices.reshape(4, 2, 4, 2, 2), ALL)
    in_specs = (
        P(ALL, None),
        P(),
        P(ALL),
        P(ALL, None),
        P(ALL, None),
        P(ALL, None, None),
        P(EXPERT, None, None),
        P(ALL, None),
        P(ALL, None),
    )
    out_specs = (P(ALL, None, None), P(EXPERT, DP, None), P(ALL, None))
    return jax.shard_map(
        on_device, mesh=torus, in_specs=in_specs, out_specs=out_specs, check_vma=False
    )
```

time: 504 us -> 119 us (0.24)
  waiting for transfers between devices: 364 us -> 0 us
  Pallas kernels: 0 us -> 114 us
  local copies, waits for them, and re-layouts: 51.8 us -> 3.25 us
  matrix products: 30 us -> 0 us
  starting transfers between devices: 20.3 us -> 0 us
  between operations: 16.4 us -> 1.29 us
  other arithmetic: 11.3 us -> 0 us
  blocking collectives: 8.37 us -> 0 us
    all_gather x1 -> x0, waiting for transfers between devices: 275 us -> none  [on_device(): lax.all_gather(masked_grad, DP_EXPERT, axis=0, tiled=True)]
    pallas_call x0 -> x1, Pallas kernels: none -> 114 us  [exchange(): pl.pallas_call(body, out_shape=(v((pairs, hid), BF), v((frows, d), F32),...]
    all_to_all x3 -> x0, waiting for transfers between devices: 89.1 us -> none  [the longest x1 73.3 us: side_by_side(): lax.all_to_all(both, axis, split_axis=split_dim, concat_axis=concat_dim,...]
    dot_general x3 -> x0, matrix products: 30 us -> none  [the longest x1 15.7 us: on_device(): lax.dot_general(arrived_hidden, arrived_grad, (((0,), (0,)), ((), ())), p...]
    all_to_all x3 -> x0, starting transfers between devices: 20 us -> none  [the longest x2 13.4 us: moved_by_axis(): result = lax.all_to_all(result, axes[k], k, k, tiled=True)]
    gather x5 -> x0, local copies, waits for them, and re-layouts: 12.8 us -> none  [the longest x1 6.14 us: on_device(): output_grad[source_token].astype(jnp.float32) * slot_scale[:, None]]
    reshape x4 -> x0, local copies, waits for them, and re-layouts: 10.4 us -> none  [the longest x1 7.34 us: on_device(): arrived_grad = arrived_grad.reshape(n_group * capacity, model_width)]
    all_to_all x2 -> x0, blocking collectives: 8.37 us -> none  [moved_by_axis(): result = lax.all_to_all(result, axes[k], k, k, tiled=True)]
  transfers between devices with their start and end apart: 5 -> 0, of which waited for: 3 -> 0; matrix products, arithmetic and copies ran while one was open for 12% -> 0% of each run, Pallas kernels for 0% -> 0%
where the time goes in v2:
time: 119 us
  Pallas kernels  114 us (96%)
  local copies, waits for them, and re-layouts  3.25 us (3%)
  between operations  1.29 us (1%)
    pallas_call x1, Pallas kernels, exchange(): pl.pallas_call(body, out_shape=(v((pairs, hid), BF), v((frows, d), F32),...  114 us
    unnamed x3, local copies, waits for them, and re-layouts  3.25 us

profile of v2, /device:TPU:0, one launch (start us, length us, event | category | flops | bytes accessed | tf_op | source)
XLA Modules:
  0.0 118.6 jit_solution(13446666798727868360)
XLA Ops:
  1.3 114.1 %exchange.1 = (bf16[256,1024]{1,0:T(8,128)(2,1)S(1)}, f32[128,7168]{1,0:T(8,128)S(1)}, f32[56,256]{1,0:T(8,128)S(1)}) custom-call(s32[8,32]{1,0:T(8,128)} %bitcast.10, s32[16]{0:T(128)} %refs_1_.1, s32[1]{0:T(128)S(6)} %copy.18.refs_2_, f32[8,32]{1,0:T(8,128)} %bitcast.11, bf16[32,256]{1,0:T(8,128)(2,1)} %refs_4_.1, bf16[32,7168]{1,0:T(8,128)(2,1)} %refs_5_.1, ...), custom_call_target="tpu_custom_call" | custom-call | tf_op jit(solution)/shard_map/exchange/pallas_call | solution.py:538
  115.4 0.8 copy.15
  116.1 1.8 %copy.16 = f32[1,128,7168]{2,1,0:T(8,128)} copy(f32[1,128,7168]{2,1,0:T(8,128)S(1)} %bitcast.6) | data formatting | bytes 7340032
  118.0 0.6 copy.17

commit v3 on v2

--- a/solution.py
+++ b/solution.py
@@ -14,12 +14,13 @@
 N_SLOT = 16
 BF = jnp.bfloat16
 F32 = jnp.float32
-WIDTHS = (768, 1280, 1536, 1792, 1792)
+WIDTHS = (1024, 1536, 2048, 1536, 1024)
 N_CHUNK = len(WIDTHS)
 STARTS = tuple(sum(WIDTHS[:i]) for i in range(N_CHUNK))
 PLANE = [(i, j, k) for i in range(NX) for j in range(NCORE) for k in range(NZ)]
 GROUP = [(i, j, k) for i in range(NXL) for j in range(NCORE) for k in range(NZ)]
-OWNERS = [(i, j) for i in range(NY) for j in range(NXH)]
+ORDER = (2, 1, 3, 0)
+PARTS = ((0, 1), (1, 3), (3, 4))
 
 
 def up(v, k, n):
@@ -38,8 +39,8 @@
         r[k] for k in ("hs", "hbuf", "ht", "wbuf", "acch", "hret", "rbuf")
     )
     saved, pick, pick_t, coef, flip = (r[k] for k in ("saved", "pick", "pick_t", "coef", "flip"))
-    xbuf, lsend, lbuf, dpart, dsend, drecv = (
-        r[k] for k in ("xbuf", "lsend", "lbuf", "dpart", "dsend", "drecv")
+    xbuf, xfwd, lsend, lbuf, dpart, dsend, drecv = (
+        r[k] for k in ("xbuf", "xfwd", "lsend", "lbuf", "dpart", "dsend", "drecv")
     )
 
     y = lax.axis_index("y")
@@ -49,7 +50,6 @@
     c = lax.axis_index("c")
     x = xh * NXL + xl
     slot = z * 4 + xl * 2 + c
-    dp = y * 2 + xh
     tok = g_hbm.shape[0]
     half_tok = tok // 2
     topk = ids.shape[0]
@@ -71,10 +71,10 @@
     dev_z = ({"z": zp}, {"z": zm}, {"z": z2})
     dev_y = ({"y": yp}, {"y": ym})
     sibling = {"c": 1 - c}
-    sent = []
-
-    def sems(name, *at):
-        return r[name + "_s"].at[at], r[name + "_r"].at[at]
+    classes = {}
+
+    def sems(name, at, out):
+        return r["out"].at[classes.setdefault(out, len(classes))], r[name].at[at]
 
     def remote(src, dst, pair, dev):
         return pltpu.make_async_remote_copy(
@@ -87,12 +87,15 @@
         )
 
     def send(src, dst, pair, dev):
-        d = remote(src, dst, pair, dev)
-        d.start()
-        sent.append(d)
-
-    def arrived(ref, pair, dev):
-        remote(ref, ref, pair, dev).wait_recv()
+        remote(src, dst, pair, dev).start()
+
+    def arrived(ref, name, at):
+        sem = r[name].at[at]
+        remote(ref, ref, (sem, sem), sibling).wait_recv()
+
+    def gone(ref, out):
+        sem = r["out"].at[classes[out]]
+        remote(ref, ref, (sem, sem), sibling).wait_send()
 
     def plane_dev(n):
         i, j, k = PLANE[n]
@@ -104,31 +107,35 @@
     def greet():
         for n in range(1, len(PLANE)):
             pl.semaphore_signal(barrier, inc=1, device_id=plane_dev(n)[3], device_id_type=MESH)
-        for i, j in OWNERS:
-            if i:
-                dev = {"y": up(y, i, NY), "xh": up(xh, j, NXH)}
-                pl.semaphore_signal(barrier, inc=1, device_id=dev, device_id_type=MESH)
+        for i in range(1, NY):
+            pl.semaphore_signal(barrier, inc=1, device_id={"y": up(y, i, NY)}, device_id_type=MESH)
 
     def bar():
-        pl.semaphore_wait(barrier, len(PLANE) - 1 + 2 * (NY - 1))
+        pl.semaphore_wait(barrier, len(PLANE) - 1 + NY - 1)
 
     def own_copy(ch):
         return pltpu.make_async_copy(
-            g_hbm.at[:, pl.ds(STARTS[ch], WIDTHS[ch])], gbuf[ch].at[x, c, z], r["loc"].at[ch]
+            g_hbm.at[:, pl.ds(STARTS[ch], WIDTHS[ch])], gbuf[ch].at[x, c, z], r["loc"].at[0]
         )
 
     def saved_copy():
-        return pltpu.make_async_copy(sv_hbm, saved, r["loc"].at[N_CHUNK])
-
-    def h_local():
-        return pltpu.make_async_copy(hs.at[xh, slot], hbuf.at[x, c, z], r["loc"].at[N_CHUNK + 1])
+        return pltpu.make_async_copy(sv_hbm, saved, r["loc"].at[1])
+
+    def h_local(which):
+        lo, hi = PARTS[which]
+        col = pl.ds(lo * frows, (hi - lo) * frows)
+        return pltpu.make_async_copy(
+            hs.at[xh, slot, :, col], hbuf.at[x, c, z, :, col], r["h"].at[which]
+        )
+
+    def x_cols(ty, th):
+        return x_hbm.at[:, pl.ds(pl.multiple_of((ty * 2 + th) * dcols, 128), dcols)]
 
     def d_local():
-        return pltpu.make_async_copy(
-            x_hbm.at[:, pl.ds(pl.multiple_of(dp * dcols, 128), dcols)],
-            xbuf.at[dp],
-            r["loc"].at[N_CHUNK + 2],
-        )
+        return pltpu.make_async_copy(x_cols(y, xh), xbuf.at[y, xh], r["dx"].at[0])
+
+    def f_local():
+        return pltpu.make_async_copy(x_cols(y, 1 - xh), xfwd.at[y], r["dx"].at[1])
 
     def w_copy(ch):
         return pltpu.make_async_copy(
@@ -164,8 +171,9 @@
         saved_copy().wait()
         table = pick[...].reshape(N_SLOT * tok, pairs)
         scale = coef[...].reshape(N_SLOT * tok, 128)
-        for n in range(NY):
-            rows = jnp.dot(table, saved[:, n * 256 : (n + 1) * 256], preferred_element_type=F32)
+        for n, k in enumerate(ORDER):
+            col = pl.ds(pl.multiple_of(up(y, k, NY) * NXH * frows, NXH * frows), NXH * frows)
+            rows = jnp.dot(table, saved[:, col], preferred_element_type=F32)
             for j in range(NXH):
                 scaled = (rows[:, j * frows : (j + 1) * frows] * scale).astype(BF)
                 hs[j, :, :, n * frows : (n + 1) * frows] = scaled.reshape(N_SLOT, tok, frows)
@@ -176,12 +184,15 @@
     def direct(ch):
         return ch == 0
 
+    def own_wait():
+        pltpu.make_async_copy(g_hbm, g_hbm, r["loc"].at[0]).wait()
+
     def s0(ch):
-        own_copy(ch).wait()
         for h in range(2):
             ref = gbuf[ch].at[x, c, z, :, lanes(ch, h)]
             for s in range(3 if direct(ch) else 2):
-                send(ref, ref, sems("a1", ch, h * 3 + s), (dev_x, dev_z)[h][s])
+                at = 0 if direct(ch) else ch * 4 + h * 2 + s
+                send(ref, ref, sems("a1", at, ("a", ch)), (dev_x, dev_z)[h][s])
 
     def s1(ch):
         for h in range(2):
@@ -191,9 +202,9 @@
                 else:
                     blk = gbuf[ch].at[x, c, (zm, zp)[s]]
                 dev = (dev_x, dev_z)[h][s]
-                arrived(blk.at[:, lanes(ch, h)], sems("a1", ch, h * 3 + s), dev)
+                arrived(blk.at[:, lanes(ch, h)], "a1", ch * 4 + h * 2 + s)
                 ref = blk.at[rows_of[s], lanes(ch, h)]
-                send(ref, ref, sems("a2", ch, h * 2 + s), dev)
+                send(ref, ref, sems("a2", ch, ("a", ch)), dev)
 
     def line(ch, h, other):
         if h == 0:
@@ -206,76 +217,75 @@
         return gbuf[ch].at[other, c, :, rows_of[s], lanes(ch, 1)]
 
     def s2(ch):
+        if direct(ch):
+            arrived(gbuf[ch].at[0:3, c, z], "a1", 0)
+        else:
+            arrived(gbuf[ch].at[0, c, z], "a2", ch)
         for h in range(2):
-            dev = (dev_x, dev_z)[h]
-            blk = gbuf[ch].at[x2, c, z] if h == 0 else gbuf[ch].at[x, c, z2]
-            if direct(ch):
-                for s in range(3):
-                    arrived(blk.at[:, lanes(ch, h)], sems("a1", ch, h * 3 + s), dev[s])
-            else:
-                for s in range(2):
-                    arrived(blk.at[rows_of[s], lanes(ch, h)], sems("a2", ch, h * 2 + s), dev[s])
             ref = line(ch, h, (z, x)[h])
             for s in range(2):
-                send(ref, ref, sems("b1", ch, h * 2 + s), (dev_z, dev_x)[h][s])
-            send(ref, ref, sems("dd", ch, h), sibling)
+                send(ref, ref, sems("b1", ch * 4 + h * 2 + s, ("b", ch)), (dev_z, dev_x)[h][s])
+            send(ref, ref, sems("dd", ch, ("d", ch)), sibling)
 
     def s3(ch):
         for h in range(2):
             for s in range(2):
-                i = h * 2 + s
                 other = ((zm, zp), (xm, xp))[h][s]
                 dev = (dev_z, dev_x)[h][s]
                 ref = line(ch, h, other)
-                arrived(ref, sems("b1", ch, i), dev)
+                arrived(ref, "b1", ch * 4 + h * 2 + s)
                 fwd = line_half(ch, h, other, s)
-                send(fwd, fwd, sems("b2", ch, i), dev)
-                send(ref, ref, sems("dd", ch, 2 + i), sibling)
+                send(fwd, fwd, sems("b2", ch, ("b", ch)), dev)
+                send(ref, ref, sems("dd", ch, ("d", ch)), sibling)
 
     def s4(ch):
+        arrived(gbuf[ch].at[:, c, z], "b2", ch)
         for h in range(2):
-            other = (z2, x2)[h]
-            for s in range(2):
-                dev = (dev_z, dev_x)[h][s]
-                arrived(line_half(ch, h, other, s), sems("b2", ch, h * 2 + s), dev)
-            ref = line(ch, h, other)
-            send(ref, ref, sems("dd", ch, 6 + h), sibling)
+            ref = line(ch, h, (z2, x2)[h])
+            send(ref, ref, sems("dd", ch, ("d", ch)), sibling)
 
     def s5(ch):
-        for i, h in enumerate((0, 1, 0, 0, 1, 1, 0, 1)):
-            arrived(line(ch, h, (z, x)[h]), sems("dd", ch, i), sibling)
-
-    def h_send(first, last):
+        arrived(gbuf[ch].at[:, 1 - c], "dd", ch)
+
+    def h_send(first, last, which):
         if first == 0:
-            h_local().start()
+            h_local(which).start()
+        lo, hi = PARTS[which]
+        col = pl.ds(lo * frows, (hi - lo) * frows)
         for m in range(first, last):
             n = ((m + 1) * 11) % len(PLANE)
             tx, tc, tz, dev = plane_dev(n)
             t_slot = tz * 4 + lax.rem(tx, NXL) * 2 + tc
-            send(hs.at[tx // NXL, t_slot], hbuf.at[x, c, z], sems("h", n), dev)
-
-    def h_build():
-        h_local().wait()
-        for n in range(1, len(PLANE)):
-            arrived(hbuf.at[x, c, z], sems("h", n), sibling)
+            src = hs.at[tx // NXL, t_slot, :, col]
+            send(src, hbuf.at[x, c, z, :, col], sems("h", which, "h"), dev)
+
+    def h_build(which):
+        lo, hi = PARTS[which]
+        col = pl.ds(lo * frows, (hi - lo) * frows)
+        arrived(hbuf.at[:, :, :, :, col], "h", which)
         n_tok = NCORE * NZ * tok
-        for k in range(NY):
-            col = pl.ds(pl.multiple_of(up(y, k, NY) * frows, frows), frows)
+        for k in range(lo, hi):
             for i in range(NX):
-                blk = hbuf[i, :, :, :, col].reshape(n_tok, frows)
+                blk = hbuf[i, :, :, :, k * frows : (k + 1) * frows].reshape(n_tok, frows)
                 ht[pl.ds(k * frows, frows), pl.ds(i * n_tok, n_tok)] = blk.T
 
-    def mm1(ch):
+    def mm1(ch, lo=0, hi=NY):
         def body(n, carry):
             col = pl.ds(pl.multiple_of(n * 256, 256), 256)
             g = gbuf[ch][:, :, :, :, col].reshape(len(PLANE) * tok, 256)
-            p = jnp.dot(ht[...], g, preferred_element_type=F32)
-            eg_out[:, pl.ds(pl.multiple_of(STARTS[ch] + n * 256, 256), 256)] = p[0:frows]
-            for k in range(1, NY):
-                part[ch][k - 1, :, col] = p[k * frows : (k + 1) * frows].astype(BF)
+            p = jnp.dot(ht[lo * frows : hi * frows], g, preferred_element_type=F32)
+            for k in range(lo, hi):
+                rows = p[(k - lo) * frows : (k - lo + 1) * frows]
+                if k == NY - 1:
+                    eg_out[:, pl.ds(pl.multiple_of(STARTS[ch] + n * 256, 256), 256)] = rows
+                else:
+                    part[ch][k, :, col] = rows.astype(BF)
             return carry
 
         lax.fori_loop(0, WIDTHS[ch] // 256, body, 0)
+
+    def m0(which):
+        mm1(0, *PARTS[which])
 
     def mm2(ch):
         w_copy(ch).wait()
@@ -297,25 +307,27 @@
 
     row_a, row_b = pl.ds(0, hrow), pl.ds(hrow, hrow)
 
-    def r0(ch):
+    def r0a(ch):
         p = part[ch]
-        send(p.at[1, row_b], relay[ch].at[0], sems("rs", ch, 0), dev_y[0])
-        send(p.at[1, row_a], relay[ch].at[1], sems("rs", ch, 1), dev_y[1])
-        send(p.at[0, row_a], recv_m[ch].at[row_a], sems("rs", ch, 2), dev_y[0])
-        send(p.at[2, row_b], recv_p[ch].at[row_b], sems("rs", ch, 3), dev_y[1])
+        send(p.at[0, row_b], relay[ch].at[0], sems("rs", ch * 3 + 0, ("r", ch)), dev_y[0])
+        send(p.at[0, row_a], relay[ch].at[1], sems("rs", ch * 3 + 1, ("r", ch)), dev_y[1])
+
+    def r0b(ch):
+        p = part[ch]
+        send(p.at[1, row_a], recv_m[ch].at[row_a], sems("rs", ch * 3 + 2, ("r", ch)), dev_y[0])
+        send(p.at[2, row_b], recv_p[ch].at[row_b], sems("rs", ch * 3 + 2, ("r", ch)), dev_y[1])
 
     def r1(ch):
         p = part[ch]
-        arrived(relay[ch].at[0], sems("rs", ch, 0), dev_y[0])
-        p[0, row_b] = (p[0, row_b].astype(F32) + relay[ch][0].astype(F32)).astype(BF)
-        send(p.at[0, row_b], recv_m[ch].at[row_b], sems("rs", ch, 4), dev_y[0])
-        arrived(relay[ch].at[1], sems("rs", ch, 1), dev_y[1])
+        arrived(relay[ch].at[0], "rs", ch * 3)
+        p[1, row_b] = (p[1, row_b].astype(F32) + relay[ch][0].astype(F32)).astype(BF)
+        send(p.at[1, row_b], recv_m[ch].at[row_b], sems("rs", ch * 3 + 2, ("r", ch)), dev_y[0])
+        arrived(relay[ch].at[1], "rs", ch * 3 + 1)
         p[2, row_a] = (p[2, row_a].astype(F32) + relay[ch][1].astype(F32)).astype(BF)
-        send(p.at[2, row_a], recv_p[ch].at[row_a], sems("rs", ch, 5), dev_y[1])
+        send(p.at[2, row_a], recv_p[ch].at[row_a], sems("rs", ch * 3 + 2, ("r", ch)), dev_y[1])
 
     def r2(ch):
-        for i in range(2, 6):
-            arrived(relay[ch].at[0], sems("rs", ch, i), dev_y[i % 2])
+        arrived(part[ch].at[0:2], "rs", ch * 3 + 2)
         col = pl.ds(STARTS[ch], WIDTHS[ch])
         eg_out[:, col] = eg_out[:, col] + (recv_m[ch][...].astype(F32) + recv_p[ch][...].astype(F32))
 
@@ -328,15 +340,14 @@
         hret[...] = acch[...].astype(BF).reshape(hret.shape)
         for n in range(1, len(GROUP)):
             tx, tc, tz, dev = group_dev(n)
-            send(hret.at[tx, tc, tz], rbuf.at[slot], sems("hr", n), dev)
-        rbuf[slot] = hret[xl, c, z]
+            send(hret.at[tx, tc, tz], rbuf.at[slot], sems("hr", 0, "hr"), dev)
+        pltpu.make_async_copy(hret.at[xl, c, z], rbuf.at[slot], r["hr"].at[0]).start()
 
     def table_flip():
         pick_t[...] = pick[...].reshape(N_SLOT * tok, pairs).T
 
     def hr_wait():
-        for n in range(1, len(GROUP)):
-            arrived(rbuf.at[slot], sems("hr", n), sibling)
+        arrived(rbuf, "hr", 0)
         scale = coef[...].reshape(N_SLOT * tok, 128)
         for n in range(hid // 256):
             halves = []
@@ -348,34 +359,32 @@
             back = jnp.dot(pick_t[...], rows, preferred_element_type=F32)
             hg_out[:, n * 256 : (n + 1) * 256] = back.astype(BF)
 
-    def d0(both):
-        if not both:
-            d_local().start()
-            lbuf[dp] = lsend[...]
-        for n, (i, j) in enumerate(OWNERS):
-            if n == 0 or j != both:
-                continue
-            ty, th = up(y, i, NY), up(xh, j, NXH)
-            td = ty * 2 + th
-            dev = {"y": ty, "xh": th}
-            send(
-                x_hbm.at[:, pl.ds(pl.multiple_of(td * dcols, 128), dcols)],
-                xbuf.at[dp],
-                sems("dx", n),
-                dev,
-            )
-            send(lsend, lbuf.at[dp], sems("dl", n), dev)
+    def d0a():
+        d_local().start()
+        f_local().start()
+        lbuf[y, xh] = lsend[...]
+        for i in range(1, NY):
+            ty = up(y, i, NY)
+            dev = {"y": ty}
+            send(x_cols(ty, 1 - xh), xfwd.at[y], sems("dx", 1, "dx"), dev)
+            send(lsend, lbuf.at[y, xh], sems("dl", 0, "dl"), dev)
+            send(x_cols(ty, xh), xbuf.at[y, xh], sems("dx", 0, "dx"), dev)
+
+    def d0b():
+        arrived(xfwd, "dx", 1)
+        arrived(lbuf.at[0:3, xh], "dl", 0)
+        dev = {"xh": 1 - xh}
+        send(xfwd, xbuf.at[:, xh], sems("dx", 0, "dxf"), dev)
+        send(lbuf.at[:, xh], lbuf.at[:, xh], sems("dl", 1, "dlf"), dev)
 
     def d1():
-        d_local().wait()
-        for n in range(1, len(OWNERS)):
-            arrived(xbuf.at[dp], sems("dx", n), sibling)
-            arrived(lbuf.at[dp], sems("dl", n), sibling)
-        n_tok = len(OWNERS) * tok
+        arrived(xbuf, "dx", 0)
+        arrived(lbuf.at[:, xh], "dl", 1)
+        n_tok = NY * NXH * tok
 
         def body(n, carry):
             col = pl.ds(pl.multiple_of(n * 128, 128), 128)
-            xt = xbuf[:, :, col].reshape(n_tok, 128).T
+            xt = xbuf[:, :, :, col].reshape(n_tok, 128).T
             dpart[col, :] = jnp.dot(
                 xt, lbuf[...].reshape(n_tok, lbuf.shape[-1]), preferred_element_type=F32
             )
@@ -386,17 +395,30 @@
             dsend[n] = dpart[n * drows : (n + 1) * drows].astype(BF)
         for n in range(1, len(GROUP)):
             tx, tc, tz, dev = group_dev(n)
-            send(dsend.at[tz * 4 + tx * 2 + tc], drecv.at[slot], sems("ds", n), dev)
-        drecv[slot] = dsend[slot]
+            send(dsend.at[tz * 4 + tx * 2 + tc], drecv.at[slot], sems("ds", 0, "ds"), dev)
+        pltpu.make_async_copy(dsend.at[slot], drecv.at[slot], r["ds"].at[0]).start()
 
     def d2():
-        for n in range(1, len(GROUP)):
-            arrived(drecv.at[slot], sems("ds", n), sibling)
+        arrived(drecv, "ds", 0)
         mine = dpart[pl.ds(pl.multiple_of(slot * drows, 8), drows)]
         total = mine - drecv[slot].astype(F32)
         for n in range(len(GROUP)):
             total = total + drecv[n].astype(F32)
         dg_out[...] = total
+
+    def sendwait():
+        for ch in range(N_CHUNK):
+            gone(gbuf[ch].at[0:3, c, z], ("a", ch))
+            gone(gbuf[ch].at[0:3, c], ("b", ch))
+            gone(gbuf[ch].at[:, c], ("d", ch))
+            gone(part[ch], ("r", ch))
+        gone(ht.at[0 : ht.shape[0] // 32 * 31], "h")
+        gone(wbuf.at[0, pl.ds(0, (len(GROUP) - 1) * tok), pl.ds(0, hid)], "hr")
+        gone(dsend.at[0 : N_SLOT - 1], "ds")
+        gone(xbuf.at[0:3], "dx")
+        gone(xfwd, "dxf")
+        gone(lbuf.at[0:3, xh], "dl")
+        gone(lbuf.at[:, xh], "dlf")
 
     greet()
     saved_copy().start()
@@ -408,74 +430,92 @@
     w_copy(0).start()
     w_copy(1).start()
     prep()
+    own_wait()
     bar()
+    h_send(24, 31, 0)
+    h_send(8, 16, 1)
+    h_send(0, 8, 1)
     s0(0)
-    h_send(0, 7)
+    s0(1)
+    h_send(16, 24, 0)
+    h_send(24, 31, 1)
     s2(0)
-    s0(1)
-    h_send(7, 15)
+    h_send(0, 8, 0)
+    h_send(16, 24, 1)
+    s1(1)
+    d0a()
     s3(0)
-    h_send(15, 31)
-    s1(1)
+    h_send(8, 16, 0)
+    table_flip()
+    s0(3)
+    s0(2)
+    h_send(16, 24, 2)
+    h_build(1)
+    s2(1)
+    h_send(24, 31, 2)
     s4(0)
-    s2(1)
-    s0(2)
-    table_flip()
-    h_build()
+    s1(2)
     s5(0)
-    mm1(0)
-    r0(0)
-    d0(0)
-    s0(3)
+    h_send(0, 8, 2)
+    h_build(0)
+    m0(0)
+    r0a(0)
+    h_send(8, 16, 2)
+    s3(1)
+    m0(1)
+    s2(2)
+    r0b(0)
+    r1(0)
+    mm2(0)
     s0(4)
-    s1(2)
-    s3(1)
-    s2(2)
+    s1(3)
+    h_build(2)
     s4(1)
-    mm2(0)
-    s1(3)
+    m0(2)
     s5(1)
     mm1(1)
-    r0(1)
+    r0a(1)
+    r0b(1)
     s3(2)
+    mm2(1)
+    s1(4)
     s2(3)
-    s1(4)
     s4(2)
-    mm2(1)
-    r1(0)
-    s3(3)
     s2(4)
     s5(2)
+    r1(1)
     mm1(2)
-    r0(2)
+    s3(3)
+    r0b(2)
+    r0a(2)
+    r2(0)
+    s3(4)
+    mm2(2)
     s4(3)
-    mm2(2)
-    s3(4)
-    d0(1)
+    s4(4)
+    d0b()
     s5(3)
     mm1(3)
-    r0(3)
-    r1(1)
-    s4(4)
+    s5(4)
+    r0a(3)
     mm2(3)
-    s5(4)
-    mm1(4)
-    r0(4)
+    r0b(3)
     mm2(4)
     hr_send()
+    d1()
     r1(2)
-    d1()
-    r2(0)
     r2(1)
+    mm1(4)
+    r0b(4)
+    r0a(4)
     r1(3)
     r2(2)
+    r1(4)
+    r2(3)
+    d2()
     hr_wait()
-    r1(4)
-    d2()
-    r2(3)
     r2(4)
-    for d in sent:
-        d.wait_send()
+    sendwait()
 
 
 def exchange(ids, home, live, gates, lat, g, sv, w, xin):
@@ -507,14 +547,13 @@
         "pick_t": v((pairs, N_SLOT * tok), BF),
         "coef": v((N_SLOT, tok, 128), F32),
         "flip": v((2, 128, 128), F32),
-        "xbuf": v((8, tok, d // 8), BF),
+        "xbuf": v((NY, NXH, tok, d // 8), BF),
+        "xfwd": v((NY, tok, d // 8), BF),
         "lsend": v((tok, kvr), BF),
-        "lbuf": v((8, tok, kvr), BF),
+        "lbuf": v((NY, NXH, tok, kvr), BF),
         "dpart": v((d // 8, kvr), F32),
         "dsend": v((N_SLOT, drows, kvr), BF),
         "drecv": v((N_SLOT, drows, kvr), BF),
-        "loc": dma((N_CHUNK + 3,)),
-        "w_sem": dma((2,)),
     }
     for i, width in enumerate(WIDTHS):
         scratch["gbuf" + str(i)] = v((NX, NCORE, NZ, tok, width), BF)
@@ -522,14 +561,13 @@
         scratch["relay" + str(i)] = v((2, frows // 2, width), BF)
         scratch["recv_p" + str(i)] = v((frows, width), BF)
         scratch["recv_m" + str(i)] = v((frows, width), BF)
-    pairs_of = {
-        "a1": (N_CHUNK, 6), "a2": (N_CHUNK, 4), "b1": (N_CHUNK, 4), "b2": (N_CHUNK, 4),
-        "dd": (N_CHUNK, 8), "h": (32,), "rs": (N_CHUNK, 6), "hr": (16,), "dx": (8,),
-        "dl": (8,), "ds": (16,),
+    counts = {
+        "a1": N_CHUNK * 4, "a2": N_CHUNK, "b1": N_CHUNK * 4, "b2": N_CHUNK, "dd": N_CHUNK,
+        "h": len(PARTS), "rs": N_CHUNK * 3, "hr": 1, "dx": 2, "dl": 2, "ds": 1,
+        "loc": 2, "w_sem": 2, "out": N_CHUNK * 4 + 7,
     }
-    for name, shape in pairs_of.items():
-        scratch[name + "_s"] = dma(shape)
-        scratch[name + "_r"] = dma(shape)
+    for name, count in counts.items():
+        scratch[name] = dma((count,))
     names = tuple(ins) + outs + tuple(scratch)
 
     def body(*refs):

time: 119 us -> 105 us (0.88)
  Pallas kernels: 114 us -> 99.5 us
    pallas_call x1, Pallas kernels: 114 us -> 99.5 us  [exchange(): pl.pallas_call(body, out_shape=(v((pairs, hid), BF), v((frows, d), F32),...]
where the time goes in v3:
time: 105 us; the launch traced here: 104 us
  Pallas kernels  99.5 us (95%)
  local copies, waits for them, and re-layouts  3.25 us (3%)
  between operations  1.29 us (1%)
    pallas_call x1, Pallas kernels, exchange(): pl.pallas_call(body, out_shape=(v((pairs, hid), BF), v((frows, d), F32),...  99.5 us
    unnamed x3, local copies, waits for them, and re-layouts  3.25 us

profile of v3, /device:TPU:0, one launch (start us, length us, event | category | flops | bytes accessed | tf_op | source)
XLA Modules:
  0.0 104.0 jit_solution(10657780559117774987)
XLA Ops:
  1.3 99.5 %exchange.1 = (bf16[256,1024]{1,0:T(8,128)(2,1)S(1)}, f32[128,7168]{1,0:T(8,128)S(1)}, f32[56,256]{1,0:T(8,128)S(1)}) custom-call(s32[8,32]{1,0:T(8,128)} %bitcast.10, s32[16]{0:T(128)} %refs_1_.1, s32[1]{0:T(128)S(6)} %copy.18.refs_2_, f32[8,32]{1,0:T(8,128)} %bitcast.11, bf16[32,256]{1,0:T(8,128)(2,1)} %refs_4_.1, bf16[32,7168]{1,0:T(8,128)(2,1)} %refs_5_.1, ...), custom_call_target="tpu_custom_call" | custom-call | tf_op jit(solution)/shard_map/exchange/pallas_call | solution.py:576
  100.7 0.8 copy.15
  101.5 1.8 %copy.16 = f32[1,128,7168]{2,1,0:T(8,128)} copy(f32[1,128,7168]{2,1,0:T(8,128)S(1)} %bitcast.6) | data formatting | bytes 7340032
  103.4 0.6 copy.17

commit v4 on v3

--- a/solution.py
+++ b/solution.py
@@ -39,8 +39,8 @@
         r[k] for k in ("hs", "hbuf", "ht", "wbuf", "acch", "hret", "rbuf")
     )
     saved, pick, pick_t, coef, flip = (r[k] for k in ("saved", "pick", "pick_t", "coef", "flip"))
-    xbuf, xfwd, lsend, lbuf, dpart, dsend, drecv = (
-        r[k] for k in ("xbuf", "xfwd", "lsend", "lbuf", "dpart", "dsend", "drecv")
+    xbuf, xfwd, xrel, lsend, lbuf, dpart, dsend, drecv = (
+        r[k] for k in ("xbuf", "xfwd", "xrel", "lsend", "lbuf", "dpart", "dsend", "drecv")
     )
 
     y = lax.axis_index("y")
@@ -373,9 +373,15 @@
     def d0b():
         arrived(xfwd, "dx", 1)
         arrived(lbuf.at[0:3, xh], "dl", 0)
-        dev = {"xh": 1 - xh}
-        send(xfwd, xbuf.at[:, xh], sems("dx", 0, "dxf"), dev)
-        send(lbuf.at[:, xh], lbuf.at[:, xh], sems("dl", 1, "dlf"), dev)
+        for s in range(2):
+            send(xfwd.at[2 * s : 2 * s + 2], xrel.at[s], sems("xr", s, "dxf"), dev_x[s])
+        send(lbuf.at[:, xh], lbuf.at[:, xh], sems("dl", 1, "dlf"), {"xh": 1 - xh})
+
+    def d0c():
+        for s in range(2):
+            arrived(xrel.at[s], "xr", s)
+            dst = xbuf.at[pl.ds(2 * s, 2), (xm, xp)[s] // NXL]
+            send(xrel.at[s], dst, sems("dx", 0, "dxf"), dev_x[s])
 
     def d1():
         arrived(xbuf, "dx", 0)
@@ -416,7 +422,7 @@
         gone(wbuf.at[0, pl.ds(0, (len(GROUP) - 1) * tok), pl.ds(0, hid)], "hr")
         gone(dsend.at[0 : N_SLOT - 1], "ds")
         gone(xbuf.at[0:3], "dx")
-        gone(xfwd, "dxf")
+        gone(xbuf, "dxf")
         gone(lbuf.at[0:3, xh], "dl")
         gone(lbuf.at[:, xh], "dlf")
 
@@ -432,84 +438,85 @@
     prep()
     own_wait()
     bar()
+    h_send(16, 24, 0)
+    s0(1)
+    h_send(16, 24, 2)
     h_send(24, 31, 0)
+    s0(0)
     h_send(8, 16, 1)
+    table_flip()
+    h_send(16, 24, 1)
+    h_send(0, 8, 0)
+    d0a()
+    h_send(8, 16, 0)
+    s2(0)
+    s0(2)
     h_send(0, 8, 1)
-    s0(0)
-    s0(1)
-    h_send(16, 24, 0)
+    s1(1)
     h_send(24, 31, 1)
-    s2(0)
-    h_send(0, 8, 0)
-    h_send(16, 24, 1)
-    s1(1)
-    d0a()
     s3(0)
-    h_send(8, 16, 0)
-    table_flip()
-    s0(3)
-    s0(2)
-    h_send(16, 24, 2)
+    h_build(0)
+    s2(1)
+    h_send(0, 8, 2)
     h_build(1)
-    s2(1)
-    h_send(24, 31, 2)
+    h_send(8, 16, 2)
+    s1(2)
     s4(0)
-    s1(2)
     s5(0)
-    h_send(0, 8, 2)
-    h_build(0)
     m0(0)
     r0a(0)
-    h_send(8, 16, 2)
+    h_send(24, 31, 2)
+    m0(1)
     s3(1)
-    m0(1)
+    s0(3)
     s2(2)
-    r0b(0)
-    r1(0)
     mm2(0)
     s0(4)
-    s1(3)
+    r0b(0)
+    s4(1)
     h_build(2)
-    s4(1)
-    m0(2)
+    r1(0)
     s5(1)
     mm1(1)
+    s1(3)
     r0a(1)
-    r0b(1)
     s3(2)
-    mm2(1)
     s1(4)
     s2(3)
+    r0b(1)
+    mm2(1)
     s4(2)
+    r1(1)
+    m0(2)
+    r2(0)
     s2(4)
     s5(2)
-    r1(1)
     mm1(2)
     s3(3)
+    r0a(2)
     r0b(2)
-    r0a(2)
-    r2(0)
-    s3(4)
     mm2(2)
     s4(3)
-    s4(4)
+    s3(4)
     d0b()
     s5(3)
     mm1(3)
-    s5(4)
-    r0a(3)
+    s4(4)
+    d0c()
     mm2(3)
     r0b(3)
+    s5(4)
     mm2(4)
     hr_send()
-    d1()
-    r1(2)
     r2(1)
     mm1(4)
+    r0a(3)
+    r1(2)
     r0b(4)
+    d1()
+    r2(2)
     r0a(4)
     r1(3)
-    r2(2)
     r1(4)
     r2(3)
     d2()
@@ -549,6 +556,7 @@
         "flip": v((2, 128, 128), F32),
         "xbuf": v((NY, NXH, tok, d // 8), BF),
         "xfwd": v((NY, tok, d // 8), BF),
+        "xrel": v((2, NY // 2, tok, d // 8), BF),
         "lsend": v((tok, kvr), BF),
         "lbuf": v((NY, NXH, tok, kvr), BF),
         "dpart": v((d // 8, kvr), F32),
@@ -563,7 +571,7 @@
         scratch["recv_m" + str(i)] = v((frows, width), BF)
     counts = {
         "a1": N_CHUNK * 4, "a2": N_CHUNK, "b1": N_CHUNK * 4, "b2": N_CHUNK, "dd": N_CHUNK,
-        "h": len(PARTS), "rs": N_CHUNK * 3, "hr": 1, "dx": 2, "dl": 2, "ds": 1,
+        "h": len(PARTS), "rs": N_CHUNK * 3, "hr": 1, "dx": 2, "xr": 2, "dl": 2, "ds": 1,
         "loc": 2, "w_sem": 2, "out": N_CHUNK * 4 + 7,
     }
     for name, count in counts.items():
@@ -588,6 +596,35 @@
         ),
         name="exchange",
     )(ids, home, live, gates, lat, g, sv, w, xin)
+
+
+def leave(hg, eg, dg):
+    pieces = 4
+    step = eg.shape[0] // pieces
+
+    def body(hg_in, eg_in, dg_in, hg_out, eg_out, dg_out, sem):
+        copies = [
+            pltpu.make_async_copy(
+                eg_in.at[pl.ds(i * step, step)], eg_out.at[pl.ds(i * step, step)], sem.at[i]
+            )
+            for i in range(pieces)
+        ]
+        copies.append(pltpu.make_async_copy(hg_in, hg_out, sem.at[pieces]))
+        copies.append(pltpu.make_async_copy(dg_in, dg_out, sem.at[pieces + 1]))
+        for copy in copies:
+            copy.start()
+        for copy in copies:
+            copy.wait()
+
+    return pl.pallas_call(
+        body,
+        out_shape=tuple(jax.ShapeDtypeStruct(a.shape, a.dtype) for a in (hg, eg, dg)),
+        in_specs=[pl.BlockSpec(memory_space=pltpu.VMEM)] * 3,
+        out_specs=(pl.BlockSpec(memory_space=pl.ANY),) * 3,
+        scratch_shapes=[pltpu.SemaphoreType.DMA((pieces + 2,))],
+        compiler_params=pltpu.CompilerParams(vmem_limit_bytes=1024 * 1024),
+        name="leave",
+    )(hg, eg, dg)
 
 
 def on_device(
@@ -614,6 +651,7 @@
         down_weight[0],
         dense_input,
     )
+    hg, eg, dg = leave(hg, eg, dg)
     return hg.reshape(tok, topk, hid), eg[None], dg
 
 

time: 105 us -> 103 us (0.981)
  local copies, waits for them, and re-layouts: 3.25 us -> 0 us
  Pallas kernels: 99.5 us -> 102 us
    unnamed x3 -> x0, local copies, waits for them, and re-layouts: 3.25 us -> none
    pallas_call x0 -> x1, Pallas kernels: none -> 2.06 us  [leave(): pl.pallas_call(body, out_shape=tuple((jax.ShapeDtypeStruct(a.shape, a.dty...]
where the time goes in v4:
time: 103 us
  Pallas kernels  102 us (99%)
  between operations  1.29 us (1%)
    pallas_call x1, Pallas kernels, exchange(): pl.pallas_call(body, out_shape=(v((pairs, hid), BF), v((frows, d), F32),...  99.6 us

profile of v4, /device:TPU:0, one launch (start us, length us, event | category | flops | bytes accessed | tf_op | source)
XLA Modules:
  0.0 102.9 jit_solution(3729869627814585349)
XLA Ops:
  1.3 99.6 %exchange.1 = (bf16[256,1024]{1,0:T(8,128)(2,1)S(1)}, f32[128,7168]{1,0:T(8,128)S(1)}, f32[56,256]{1,0:T(8,128)S(1)}) custom-call(s32[8,32]{1,0:T(8,128)} %bitcast.8, s32[16]{0:T(128)} %refs_1_.1, s32[1]{0:T(128)S(6)} %copy.12.refs_2_, f32[8,32]{1,0:T(8,128)} %bitcast.9, bf16[32,256]{1,0:T(8,128)(2,1)} %refs_4_.1, bf16[32,7168]{1,0:T(8,128)(2,1)} %refs_5_.1, ...), custom_call_target="tpu_custom_call" | custom-call | tf_op jit(solution)/shard_map/exchange/pallas_call | solution.py:584
  100.9 2.1 %leave.1 = (bf16[256,1024]{1,0:T(8,128)(2,1)}, f32[128,7168]{1,0:T(8,128)}, f32[56,256]{1,0:T(8,128)}) custom-call(bf16[256,1024]{1,0:T(8,128)(2,1)S(1)} %get-tuple-element.9.hg_in, f32[128,7168]{1,0:T(8,128)S(1)} %get-tuple-element.10.eg_in, f32[56,256]{1,0:T(8,128)S(1)} %get-tuple-element.11.dg_in), custom_call_target="tpu_custom_call" | custom-call | tf_op jit(solution)/shard_map/leave/pallas_call | solution.py:619

commit v5 on v4

--- a/solution.py
+++ b/solution.py
@@ -501,22 +501,22 @@
     d0b()
     s5(3)
     mm1(3)
+    r0a(3)
+    r0b(3)
     s4(4)
     d0c()
     mm2(3)
-    r0b(3)
     s5(4)
+    mm1(4)
+    r0a(4)
+    r0b(4)
     mm2(4)
     hr_send()
+    r1(2)
+    d1()
+    r1(3)
     r2(1)
-    mm1(4)
-    r0a(3)
-    r1(2)
-    r0b(4)
-    d1()
     r2(2)
-    r0a(4)
-    r1(3)
     r1(4)
     r2(3)
     d2()

time: 103 us -> 102 us (level)
  Pallas kernels: 102 us -> 99.7 us
    pallas_call x1, Pallas kernels: 99.6 us -> 97.6 us  [exchange(): pl.pallas_call(body, out_shape=(v((pairs, hid), BF), v((frows, d), F32),...]
where the time goes in v5:
time: 102 us; the launch traced here: 101 us
  Pallas kernels  99.7 us (98%)
  between operations  1.29 us (1%)
    pallas_call x1, Pallas kernels, exchange(): pl.pallas_call(body, out_shape=(v((pairs, hid), BF), v((frows, d), F32),...  97.6 us
    pallas_call x1, Pallas kernels, leave(): pl.pallas_call(body, out_shape=tuple((jax.ShapeDtypeStruct(a.shape, a.dty...  2.06 us

profile of v5, /device:TPU:0, one launch (start us, length us, event | category | flops | bytes accessed | tf_op | source)
XLA Modules:
  0.0 101.0 jit_solution(9338082758535584368)
XLA Ops:
  1.3 97.6 %exchange.1 = (bf16[256,1024]{1,0:T(8,128)(2,1)S(1)}, f32[128,7168]{1,0:T(8,128)S(1)}, f32[56,256]{1,0:T(8,128)S(1)}) custom-call(s32[8,32]{1,0:T(8,128)} %bitcast.8, s32[16]{0:T(128)} %refs_1_.1, s32[1]{0:T(128)S(6)} %copy.12.refs_2_, f32[8,32]{1,0:T(8,128)} %bitcast.9, bf16[32,256]{1,0:T(8,128)(2,1)} %refs_4_.1, bf16[32,7168]{1,0:T(8,128)(2,1)} %refs_5_.1, ...), custom_call_target="tpu_custom_call" | custom-call | tf_op jit(solution)/shard_map/exchange/pallas_call | solution.py:584
  98.9 2.1 %leave.1 = (bf16[256,1024]{1,0:T(8,128)(2,1)}, f32[128,7168]{1,0:T(8,128)}, f32[56,256]{1,0:T(8,128)}) custom-call(bf16[256,1024]{1,0:T(8,128)(2,1)S(1)} %get-tuple-element.9.hg_in, f32[128,7168]{1,0:T(8,128)S(1)} %get-tuple-element.10.eg_in, f32[56,256]{1,0:T(8,128)S(1)} %get-tuple-element.11.dg_in), custom_call_target="tpu_custom_call" | custom-call | tf_op jit(solution)/shard_map/leave/pallas_call | solution.py:619

commit v6 on v5

--- a/solution.py
+++ b/solution.py
@@ -14,7 +14,7 @@
 N_SLOT = 16
 BF = jnp.bfloat16
 F32 = jnp.float32
-WIDTHS = (1024, 1536, 2048, 1536, 1024)
+WIDTHS = (1536, 1536, 1792, 1280, 1024)
 N_CHUNK = len(WIDTHS)
 STARTS = tuple(sum(WIDTHS[:i]) for i in range(N_CHUNK))
 PLANE = [(i, j, k) for i in range(NX) for j in range(NCORE) for k in range(NZ)]
@@ -438,41 +438,41 @@
     prep()
     own_wait()
     bar()
+    s0(0)
+    h_send(0, 8, 0)
+    h_send(8, 16, 0)
     h_send(16, 24, 0)
+    h_send(24, 31, 0)
     s0(1)
-    h_send(16, 24, 2)
-    h_send(24, 31, 0)
-    s0(0)
+    d0a()
+    table_flip()
+    s2(0)
+    h_send(0, 8, 1)
     h_send(8, 16, 1)
-    table_flip()
     h_send(16, 24, 1)
-    h_send(0, 8, 0)
-    d0a()
-    h_send(8, 16, 0)
-    s2(0)
     s0(2)
-    h_send(0, 8, 1)
     s1(1)
+    s3(0)
     h_send(24, 31, 1)
-    s3(0)
-    h_build(0)
+    s4(0)
     s2(1)
     h_send(0, 8, 2)
-    h_build(1)
     h_send(8, 16, 2)
-    s1(2)
-    s4(0)
+    h_build(0)
     s5(0)
     m0(0)
     r0a(0)
+    h_build(1)
+    m0(1)
+    r0b(0)
+    s1(2)
+    h_send(16, 24, 2)
     h_send(24, 31, 2)
-    m0(1)
     s3(1)
     s0(3)
     s2(2)
     mm2(0)
     s0(4)
-    r0b(0)
     s4(1)
     h_build(2)
     r1(0)

time: 102 us -> 101 us (level)
  Pallas kernels: 99.7 us -> 98.5 us
    pallas_call x1, Pallas kernels: 97.6 us -> 96.4 us  [exchange(): pl.pallas_call(body, out_shape=(v((pairs, hid), BF), v((frows, d), F32),...]
where the time goes in v6:
time: 101 us; the launch traced here: 99.8 us
  Pallas kernels  98.5 us (98%)
  between operations  1.29 us (1%)
    pallas_call x1, Pallas kernels, exchange(): pl.pallas_call(body, out_shape=(v((pairs, hid), BF), v((frows, d), F32),...  96.4 us
    pallas_call x1, Pallas kernels, leave(): pl.pallas_call(body, out_shape=tuple((jax.ShapeDtypeStruct(a.shape, a.dty...  2.06 us

profile of v6, /device:TPU:0, one launch (start us, length us, event | category | flops | bytes accessed | tf_op | source)
XLA Modules:
  0.0 99.8 jit_solution(14340249113002540787)
XLA Ops:
  1.3 96.4 %exchange.1 = (bf16[256,1024]{1,0:T(8,128)(2,1)S(1)}, f32[128,7168]{1,0:T(8,128)S(1)}, f32[56,256]{1,0:T(8,128)S(1)}) custom-call(s32[8,32]{1,0:T(8,128)} %bitcast.8, s32[16]{0:T(128)} %refs_1_.1, s32[1]{0:T(128)S(6)} %copy.12.refs_2_, f32[8,32]{1,0:T(8,128)} %bitcast.9, bf16[32,256]{1,0:T(8,128)(2,1)} %refs_4_.1, bf16[32,7168]{1,0:T(8,128)(2,1)} %refs_5_.1, ...), custom_call_target="tpu_custom_call" | custom-call | tf_op jit(solution)/shard_map/exchange/pallas_call | solution.py:584
  97.7 2.1 %leave.1 = (bf16[256,1024]{1,0:T(8,128)(2,1)}, f32[128,7168]{1,0:T(8,128)}, f32[56,256]{1,0:T(8,128)}) custom-call(bf16[256,1024]{1,0:T(8,128)(2,1)S(1)} %get-tuple-element.9.hg_in, f32[128,7168]{1,0:T(8,128)S(1)} %get-tuple-element.10.eg_in, f32[56,256]{1,0:T(8,128)S(1)} %get-tuple-element.11.dg_in), custom_call_target="tpu_custom_call" | custom-call | tf_op jit(solution)/shard_map/leave/pallas_call | solution.py:619
